TPU v7x, 32 devices: a whole 2x2x4 slice. The times are simulated.
32 devices in a mesh: section: 8 (over z, y), state: 4 (over x, core).
Axes of the slice: x: 2, y: 2, z: 4, core: 2. Of those that a mesh axis runs over, the one named last changes fastest.
Arguments:
- initial_state: float32 [32, 1024], P('state'), may hold values from -6 to 6
- state_ref: float32 [192, 32, 1024], P('section', 'state'), may hold values from -6 to 6
- state_weight: float32 [192, 32, 1024], P('section', 'state'), may hold values from 0.2 to 5
- input_matrix: bfloat16 [32, 1024, 512], P('state'), may hold values from -0.25 to 0.25
- kkt_inverse: float32 [512, 512], replicated, may hold values from -1 to 1, as said below
- input_bound: float32 [512], replicated, may hold values from 0.02 to 0.3
Outputs:
- states: float32 [192, 32, 1024], P('section', 'state')
- boxed: float32 [192, 512], P('section')
- dual_vars: float32 [192, 32, 1024], P('section', 'state')
- history: float32 [10, 2], replicated
Inputs may be any that keep to these rules, and one draw needn't show every extreme that they name: `kkt_inverse`: a symmetric matrix.
All inputs are finite; a program needn't handle non-finite values.
Results may differ from a plain program's by a relative error of at most 0.003.
Values may be sent and summed in bfloat16 or wider, within the bound.
No kernel may reach another device: no remote copies, remote signals or barrier semaphores. Data moves between devices by JAX's collectives and lax.ppermute only.
A program may use at most 128 MiB of HBM per device.

v0:
```python
import jax
import jax.numpy as jnp
from jax import lax
from jax.sharding import PartitionSpec as P

GX = 32
GY = 32
GZ = 32
ITERS = 10


diffusion = 0.15
epsilon = 1e-06


def with_halo(block, sides, width):
    for axis, dim in sides:
        count = lax.axis_size(axis)
        forward = [(i, i + 1) for i in range(count - 1)]
        backward = [(target, source) for source, target in forward]
        low = lax.ppermute(
            lax.slice_in_dim(block, block.shape[dim] - width, None, axis=dim), axis, forward
        )
        high = lax.ppermute(lax.slice_in_dim(block, 0, width, axis=dim), axis, backward)
        block = jnp.concatenate([low, block, high], axis=dim)
    return block


def passed_along(value, axis, steps):
    count = lax.axis_size(axis)
    leading, last = (max(0, -steps), min(count, count - steps))
    return lax.ppermute(value, axis, [(source, source + steps) for source in range(leading, last)])


def stencil(padded):
    centre = padded[:, 1:-1]
    across = padded[:, 2:] + padded[:, :-2]
    depth = centre.shape[-1]
    flat_pad = jnp.pad(centre, ((0, 0), (0, 0), (GZ, GZ)))
    along_y = flat_pad[:, :, 2 * GZ :] + flat_pad[:, :, : -2 * GZ]
    lower_z = jnp.pad(centre, ((0, 0), (0, 0), (1, 0)))[:, :, :-1]
    upper_z = jnp.pad(centre, ((0, 0), (0, 0), (0, 1)))[:, :, 1:]
    z_index = jnp.arange(depth) % GZ
    along_z = jnp.where(z_index > 0, lower_z, 0.0) + jnp.where(z_index < GZ - 1, upper_z, 0.0)
    return centre + diffusion * (across + along_y + along_z - 6.0 * centre)


def apply_rows(inputs_low, matrix):
    return lax.dot_general(
        inputs_low, matrix, (((1,), (1,)), ((), ())), preferred_element_type=jnp.float32
    )


def local(initial_state, state_ref, state_weight, input_matrix, kkt_inverse, input_bound):
    section_count, planes, plane_size = state_ref.shape
    input_width = input_matrix.shape[2]
    matrix = input_matrix.reshape(planes * plane_size, input_width)
    penalty = float(GX * GY * GZ) / input_width
    is_first = lax.axis_index("section") == 0
    groups = lax.axis_size("state")
    state_seat = lax.axis_index("state")
    cell_count = section_count * lax.axis_size("section") * GX * GY * GZ
    input_count = section_count * lax.axis_size("section") * input_width
    states = jnp.zeros_like(state_ref)
    dual_vars = jnp.zeros_like(state_ref)
    boxed = jnp.zeros((section_count, input_width), jnp.float32)
    scaled = jnp.zeros((section_count, input_width), jnp.float32)
    wide_matrix = with_halo(input_matrix, (("state", 0),), 1).reshape(-1, input_width)
    plane_index = jnp.arange(planes + 2)[:, None]
    outside = (plane_index == 0) & (state_seat == 0) | (plane_index == planes + 1) & (
        state_seat == groups - 1
    )
    rim_mask = jnp.where(outside, 0.0, 1.0).astype(jnp.float32)
    history = []
    for iteration in range(ITERS):
        last_state = passed_along(states[-1], "section", 1)
        prior = jnp.where(is_first, initial_state, last_state)
        joined = jnp.concatenate([prior[None], states, dual_vars], 0)
        padded = with_halo(joined, (("state", 1),), 2)
        moved_wide = stencil(padded[:section_count])
        states_wide = padded[1 : section_count + 1, 1:-1]
        duals_wide = padded[section_count + 1 :, 1:-1]
        target_wide = states_wide - moved_wide + duals_wide
        moved_prior = moved_wide[:, 1:-1]
        target = target_wide[:, 1:-1]
        target_low = target.astype(jnp.bfloat16).reshape(section_count, -1)
        partial_pull = jnp.dot(target_low, matrix, preferred_element_type=jnp.float32)
        pulled = lax.psum(partial_pull, "state")
        rhs_rows = pulled + penalty * (boxed - scaled)
        inputs = jnp.dot(rhs_rows, kkt_inverse, precision=lax.Precision.HIGHEST)
        inputs_low = inputs.astype(jnp.bfloat16)
        driven_wide = apply_rows(inputs_low, wide_matrix).reshape(
            section_count, planes + 2, plane_size
        )
        defect_wide = (target_wide - driven_wide) * rim_mask
        driven = driven_wide[:, 1:-1]
        defect = defect_wide[:, 1:-1]
        following = passed_along(defect_wide[0], "section", -1)
        ahead_defect = jnp.concatenate([defect_wide[1:], following[None]], 0)
        back_term = stencil(ahead_defect)
        updated = (state_weight * state_ref + (states - defect) + back_term + states) / (
            state_weight + 2.0
        )
        primal = updated - moved_prior - driven
        dual_vars = dual_vars + primal
        boxed_new = jnp.clip(inputs + scaled, -input_bound, input_bound)
        box_gap = inputs - boxed_new
        scaled = scaled + box_gap
        boxed = boxed_new
        states = updated
        primal_square = jnp.sum(primal * primal)
        gap_square = jnp.sum(box_gap * box_gap) / groups
        totals = lax.psum((primal_square, gap_square), ("section", "state"))
        history.append(
            jnp.stack(
                [
                    jnp.sqrt(totals[0] / cell_count + epsilon),
                    jnp.sqrt(totals[1] / input_count + epsilon),
                ]
            )
        )
    record = jnp.stack(history)
    return (states, boxed, dual_vars, record)


def solution(mesh):
    return jax.shard_map(
        local,
        mesh=mesh,
        in_specs=(
            P("state", None),
            P("section", "state", None),
            P("section", "state", None),
            P("state", None, None),
            P(),
            P(),
        ),
        out_specs=(
            P("section", "state", None),
            P("section", None),
            P("section", "state", None),
            P(),
        ),
        check_vma=False,
    )
```

profile of v0, /device:TPU:0, one launch (start us, length us, event | category | flops | bytes accessed | tf_op | source)
XLA Modules:
  0.0 624.7 jit_solution(1933036389020178397)
XLA Ops:
  0.7 5.0 collective-permute-start
  9.6 3.1 collective-permute-start.1
  12.6 3.0 fusion.420
  15.6 4.0 collective-permute-start.3
  22.1 2.9 slice_add_fusion.4
  26.7 14.3 %psum.210 = f32[24,512]{1,0:T(8,128)S(1)} all-reduce(f32[24,512]{1,0:T(8,128)S(1)} %convolution_bitcast_fusion.9), channel_id=1, replica_groups=mesh['section'=8,'state'=4] {'state'}, use_global_device_ids=true, to_apply=%region_0.1 | all-reduce | flops 12288 | bytes 98304 | tf_op jit(solution)/shard_map/psum | solution.py:88
  44.0 7.3 %constant_dynamic-update-slice_fusion.1 = bf16[10,1024,512]{2,1,0:T(8,128)(2,1)} fusion(bf16[10,1024,512]{2,1,0:T(8,128)(2,1)} %constant_dynamic-update-slice_fusion.2, bf16[8,1024,512]{2,1,0:T(8,128)(2,1)} %param.9), kind=kLoop, calls=%fused_computation.746 | loop fusion | bytes 16777216
  53.5 6.9 %fusion.342 = f32[24,10,1024]{2,0,1:T(8,128)S(1)} fusion(bf16[10,1024,512]{2,1,0:T(8,128)(2,1)} %constant_dynamic-update-slice_fusion, f32[24,512]{1,0:T(8,128)S(1)} %fusion.421), kind=kOutput, calls=%fused_computation.705 | convolution fusion | flops 251670528 | bytes 11517952 | tf_op jit(solution)/shard_map/dot_general | solution.py:49
  63.8 4.1 collective-permute-done.5
  69.9 4.6 collective-permute-start.6
  77.8 3.1 collective-permute-start.7
  83.1 3.3 slice_add_fusion.3
  89.2 16.2 %psum.211 = f32[24,512]{1,0:T(8,128)} all-reduce(f32[24,512]{1,0:T(8,128)S(1)} %convolution_bitcast_fusion.8), channel_id=1, replica_groups=mesh['section'=8,'state'=4] {'state'}, use_global_device_ids=true, to_apply=%region_1.2 | all-reduce | flops 12288 | bytes 98304 | tf_op jit(solution)/shard_map/psum | solution.py:88
  107.5 6.9 %fusion.340 = f32[24,10,1024]{2,0,1:T(8,128)S(1)} fusion(bf16[10,1024,512]{2,1,0:T(8,128)(2,1)} %constant_dynamic-update-slice_fusion, f32[24,512]{1,0:T(8,128)S(1)} %get-tuple-element.121), kind=kOutput, calls=%fused_computation.703 | convolution fusion | flops 251670528 | bytes 11517952 | tf_op jit(solution)/shard_map/dot_general | solution.py:49
  116.8 5.2 collective-permute-done.9
  122.2 2.8 multiply_reduce_fusion.8
  125.0 4.5 collective-permute-start.10
  132.7 3.5 collective-permute-start.11
  138.0 3.3 slice_add_fusion.2
  144.1 15.6 %psum.212 = f32[24,512]{1,0:T(8,128)S(1)} all-reduce(f32[24,512]{1,0:T(8,128)S(1)} %convolution_bitcast_fusion.7), channel_id=1, replica_groups=mesh['section'=8,'state'=4] {'state'}, use_global_device_ids=true, to_apply=%region_2.3 | all-reduce | flops 12288 | bytes 98304 | tf_op jit(solution)/shard_map/psum | solution.py:88
  160.4 6.9 %fusion.338 = f32[24,10,1024]{2,0,1:T(8,128)S(1)} fusion(bf16[10,1024,512]{2,1,0:T(8,128)(2,1)} %constant_dynamic-update-slice_fusion, f32[24,512]{1,0:T(8,128)S(1)} %fusion.297), kind=kOutput, calls=%fused_computation.701 | convolution fusion | flops 251670528 | bytes 11517952 | tf_op jit(solution)/shard_map/dot_general | solution.py:49
  169.8 5.6 collective-permute-done.13
  175.6 2.8 multiply_reduce_fusion.7
  178.4 4.5 collective-permute-start.14
  186.1 3.2 collective-permute-start.15
  191.4 3.3 slice_add_fusion.1
  198.1 16.8 %psum.213 = f32[24,512]{1,0:T(8,128)} all-reduce(f32[24,512]{1,0:T(8,128)} %convolution_bitcast_fusion.6), channel_id=1, replica_groups=mesh['section'=8,'state'=4] {'state'}, use_global_device_ids=true, to_apply=%region_3.4 | all-reduce | flops 12288 | bytes 98304 | tf_op jit(solution)/shard_map/psum | solution.py:88
  217.0 6.9 %fusion.336 = f32[24,10,1024]{2,0,1:T(8,128)S(1)} fusion(bf16[10,1024,512]{2,1,0:T(8,128)(2,1)} %constant_dynamic-update-slice_fusion, f32[24,512]{1,0:T(8,128)S(1)} %get-tuple-element.123), kind=kOutput, calls=%fused_computation.699 | convolution fusion | flops 251670528 | bytes 11517952 | tf_op jit(solution)/shard_map/dot_general | solution.py:49
  226.3 5.6 collective-permute-done.17
  232.2 2.7 multiply_reduce_fusion.6
  234.9 4.5 collective-permute-start.18
  242.9 3.3 collective-permute-start.19
  248.1 3.3 slice_add_fusion
  254.3 15.6 %psum.214 = f32[24,512]{1,0:T(8,128)S(1)} all-reduce(f32[24,512]{1,0:T(8,128)S(1)} %convolution_bitcast_fusion.5), channel_id=1, replica_groups=mesh['section'=8,'state'=4] {'state'}, use_global_device_ids=true, to_apply=%region_4.5 | all-reduce | flops 12288 | bytes 98304 | tf_op jit(solution)/shard_map/psum | solution.py:88
  270.6 6.9 %fusion.334 = f32[24,10,1024]{2,0,1:T(8,128)S(1)} fusion(bf16[10,1024,512]{2,1,0:T(8,128)(2,1)} %constant_dynamic-update-slice_fusion, f32[24,512]{1,0:T(8,128)S(1)} %fusion.289), kind=kOutput, calls=%fused_computation.697 | convolution fusion | flops 251670528 | bytes 11517952 | tf_op jit(solution)/shard_map/dot_general | solution.py:49
  279.9 5.3 collective-permute-done.21
  289.7 4.5 collective-permute-start.22
  297.3 3.7 collective-permute-start.23
  306.7 17.3 %psum.215 = f32[24,512]{1,0:T(8,128)} all-reduce(f32[24,512]{1,0:T(8,128)} %convolution_bitcast_fusion.4), channel_id=1, replica_groups=mesh['section'=8,'state'=4] {'state'}, use_global_device_ids=true, to_apply=%region_5.6 | all-reduce | flops 12288 | bytes 98304 | tf_op jit(solution)/shard_map/psum | solution.py:88
  326.3 7.6 %subtract_multiply_fusion.8 = (f32[24,10,1024]{2,0,1:T(8,128)S(1)}, f32[24,10,1024]{2,0,1:T(8,128)S(1)}) fusion(f32[10]{0:T(128)} %copy-done.88, f32[49,12,1024]{2,0,1:T(8,128)} %copy-done.33, f32[24,10,1024]{2,0,1:T(8,128)S(1)} %copy-done.7, bf16[10,1024,512]{2,1,0:T(8,128)(2,1)} %constant_dynamic-update-slice_fusion, f32[24,512]{1,0:T(8,128)S(1)} %get-tuple-element.127), kind=kOutput, calls=%fused_computation.278 | convolution fusion | flops 252653568 | bytes 15450152 | tf_op jit(solution)/shard_map/dot_general | solution.py:49
  335.5 5.7 collective-permute-done.25
  341.3 2.4 multiply_reduce_fusion.4
  343.7 4.5 collective-permute-start.26
  351.3 3.3 collective-permute-start.27
  360.3 16.3 %psum.216 = f32[24,512]{1,0:T(8,128)S(1)} all-reduce(f32[24,512]{1,0:T(8,128)S(1)} %convolution_bitcast_fusion.3), channel_id=1, replica_groups=mesh['section'=8,'state'=4] {'state'}, use_global_device_ids=true, to_apply=%region_6.7 | all-reduce | flops 12288 | bytes 98304 | tf_op jit(solution)/shard_map/psum | solution.py:88
  377.9 7.5 %subtract_multiply_fusion.7 = (f32[24,10,1024]{2,0,1:T(8,128)S(1)}, f32[24,10,1024]{2,0,1:T(8,128)S(1)}) fusion(f32[10]{0:T(128)S(1)} %copy-done.93, f32[49,12,1024]{2,0,1:T(8,128)} %copy-done.35, f32[24,10,1024]{2,0,1:T(8,128)S(1)} %copy-done.11, bf16[10,1024,512]{2,1,0:T(8,128)(2,1)} %constant_dynamic-update-slice_fusion, f32[24,512]{1,0:T(8,128)S(1)} %fusion.281), kind=kOutput, calls=%fused_computation.277 | convolution fusion | flops 252653568 | bytes 15450152 | tf_op jit(solution)/shard_map/dot_general | solution.py:49
  387.0 5.6 collective-permute-done.29
  395.0 4.5 collective-permute-start.30
  402.6 3.3 collective-permute-start.31
  412.1 17.3 %psum.217 = f32[24,512]{1,0:T(8,128)} all-reduce(f32[24,512]{1,0:T(8,128)} %convolution_bitcast_fusion.2), channel_id=1, replica_groups=mesh['section'=8,'state'=4] {'state'}, use_global_device_ids=true, to_apply=%region_7.8 | all-reduce | flops 12288 | bytes 98304 | tf_op jit(solution)/shard_map/psum | solution.py:88
  431.7 7.6 %subtract_multiply_fusion.6 = (f32[24,10,1024]{2,0,1:T(8,128)S(1)}, f32[24,10,1024]{2,0,1:T(8,128)S(1)}) fusion(f32[10]{0:T(128)} %copy-done.88, f32[49,12,1024]{2,0,1:T(8,128)} %copy-done.34, f32[24,10,1024]{2,0,1:T(8,128)S(1)} %copy-done.9, bf16[10,1024,512]{2,1,0:T(8,128)(2,1)} %constant_dynamic-update-slice_fusion, f32[24,512]{1,0:T(8,128)S(1)} %get-tuple-element.133), kind=kOutput, calls=%fused_computation.276 | convolution fusion | flops 252653568 | bytes 15450152 | tf_op jit(solution)/shard_map/dot_general | solution.py:49
  440.7 5.7 collective-permute-done.33
  448.6 4.8 collective-permute-start.34
  456.5 3.1 collective-permute-start.35
  465.3 16.2 %psum.218 = f32[24,512]{1,0:T(8,128)S(1)} all-reduce(f32[24,512]{1,0:T(8,128)S(1)} %convolution_bitcast_fusion.1), channel_id=1, replica_groups=mesh['section'=8,'state'=4] {'state'}, use_global_device_ids=true, to_apply=%region_8.9 | all-reduce | flops 12288 | bytes 98304 | tf_op jit(solution)/shard_map/psum | solution.py:88
  482.6 7.5 %subtract_multiply_fusion.5 = (f32[24,10,1024]{2,0,1:T(8,128)S(1)}, f32[24,10,1024]{2,0,1:T(8,128)S(1)}) fusion(f32[10]{0:T(128)S(1)} %copy-done.94, f32[49,12,1024]{2,0,1:T(8,128)} %copy-done.36, f32[24,10,1024]{2,0,1:T(8,128)S(1)} %copy-done.13, bf16[10,1024,512]{2,1,0:T(8,128)(2,1)} %constant_dynamic-update-slice_fusion, f32[24,512]{1,0:T(8,128)S(1)} %fusion.273), kind=kOutput, calls=%fused_computation.275 | convolution fusion | flops 252653568 | bytes 15450152 | tf_op jit(solution)/shard_map/dot_general | solution.py:49
  491.8 5.7 collective-permute-done.37
  499.7 4.5 collective-permute-start.38
  507.6 3.1 collective-permute-start.39
  516.9 17.7 %psum.219 = f32[24,512]{1,0:T(8,128)} all-reduce(f32[24,512]{1,0:T(8,128)} %convolution_bitcast_fusion), channel_id=1, replica_groups=mesh['section'=8,'state'=4] {'state'}, use_global_device_ids=true, to_apply=%region_9.10 | all-reduce | flops 12288 | bytes 98304 | tf_op jit(solution)/shard_map/psum | solution.py:88
  534.5 3.2 multiply_reduce_fusion.12
  537.7 8.5 %subtract_multiply_fusion.4 = (f32[24,10,1024]{2,0,1:T(8,128)S(1)}, f32[24,10,1024]{2,0,1:T(8,128)}) fusion(f32[10]{0:T(128)S(1)} %copy-done.95, f32[49,12,1024]{2,0,1:T(8,128)} %copy-done.37, f32[24,10,1024]{2,0,1:T(8,128)S(1)} %copy-done.15, bf16[10,1024,512]{2,1,0:T(8,128)(2,1)} %constant_dynamic-update-slice_fusion, ...), kind=kOutput, calls=%fused_computation.274 | convolution fusion | flops 252641280 | bytes 15425576 | tf_op jit(solution)/shard_map/dot_general | solution.py:49
  557.0 3.8 multiply_reduce_fusion
  563.7 44.8 %all-reduce.61 = (f32[]{:T(128)}, f32[]{:T(128)}, f32[]{:T(128)}, f32[]{:T(128)}, f32[]{:T(128)}, /*index=5*/f32[]{:T(128)}, f32[]{:T(128)}, f32[]{:T(128)}, f32...) all-reduce(f32[]{:T(128)S(6)} %div.131, ...), channel_id=1, replica_groups=mesh['section'=8,'state'=4] {'section','state'}, use_global_device_ids=true, to_apply=%region_13.14 | all-reduce | flops 20 | bytes 160 | tf_op jit(solution)/shard_map/psum | solution.py:113
  (480 shorter events, 145.0 us)
Async XLA Ops:
  0.6 40.4 %copy-start = (f32[512,512]{1,0:T(8,128)S(1)}, f32[512,512]{1,0:T(8,128)}, u32[]{:S(2)}) copy-start(f32[512,512]{1,0:T(8,128)} %param.10) | copy-start | bytes 3145732
  0.7 6.6 %collective-permute-start = (f32[8,1024]{1,0:T(8,128)S(1)}, f32[8,1024]{1,0:T(8,128)S(1)}, u32[]{:S(2)}, u32[]{:S(2)}) collective-permute-start(f32[8,1024]{1,0:T(8,128)S(1)} %squeeze.60), channel_id=1, source_target_pairs={{0,4},{4,8},{8,12},{12,16},{16,20},{20,24},{24,28},{1,5},{5,9},{9,... | collective-permute-start | bytes 98312 | tf_op jit(solution)/shard_map/ppermute | solution.py:32
  8.3 12.9 %collective-permute-start.2 = (f32[49,2,1024]{2,1,0:T(2,128)S(1)}, f32[49,2,1024]{2,1,0:T(2,128)S(1)}, u32[]{:S(2)}, u32[]{:S(2)}) collective-permute-start(f32[49,2,1024]{2,1,0:T(2,128)S(1)} %get-tuple-element.119), channel_id=1, source_target_pairs={{1,0},{2,1},{3,2},{5,4},{6,5},{7,6},{9,8},{10,9},{11,10},{13,12},{... | collective-permute-start | bytes 1204232 | tf_op jit(solution)/shard_map/ppermute | solution.py:24
  9.6 11.6 %collective-permute-start.1 = (f32[49,2,1024]{2,1,0:T(2,128)S(1)}, f32[49,2,1024]{2,1,0:T(2,128)S(1)}, u32[]{:S(2)}, u32[]{:S(2)}) collective-permute-start(f32[49,2,1024]{2,1,0:T(2,128)S(1)} %get-tuple-element.118), channel_id=1, source_target_pairs={{0,1},{1,2},{2,3},{4,5},{5,6},{6,7},{8,9},{9,10},{10,11},{12,13},{... | collective-permute-start | bytes 1204232 | tf_op jit(solution)/shard_map/ppermute | solution.py:21
  15.6 26.1 %collective-permute-start.3 = (bf16[1,1024,512]{2,1,0:T(8,128)(2,1)}, bf16[1,1024,512]{2,1,0:T(8,128)(2,1)}, u32[]{:S(2)}, u32[]{:S(2)}) collective-permute-start(bf16[1,1024,512]{2,1,0:T(8,128)(2,1)} %get-tuple-element.86), channel_id=1, source_target_pairs={{0,1},{1,2},{2,3},{4,5},{5,6},{6,7},{8,9},{9,10},{10,11},{12,13},{... | collective-permute-start | bytes 3145736 | tf_op jit(solution)/shard_map/ppermute | solution.py:21
  19.6 31.6 %collective-permute-start.4 = (bf16[1,1024,512]{2,1,0:T(8,128)(2,1)}, bf16[1,1024,512]{2,1,0:T(8,128)(2,1)}, u32[]{:S(2)}, u32[]{:S(2)}) collective-permute-start(bf16[1,1024,512]{2,1,0:T(8,128)(2,1)} %get-tuple-element.85), channel_id=1, source_target_pairs={{1,0},{2,1},{3,2},{5,4},{6,5},{7,6},{9,8},{10,9},{11,10},{13,12},{... | collective-permute-start | bytes 3145736 | tf_op jit(solution)/shard_map/ppermute | solution.py:24
  20.9 39.5 %copy-start.88 = (f32[10]{0:T(128)}, f32[10]{0:T(128)S(1)}, u32[]{:S(2)}) copy-start(f32[10]{0:T(128)S(1)} %or_select_fusion) | copy-start | bytes 124
  61.3 6.6 %collective-permute-start.5 = (f32[10,1024]{1,0:T(8,128)S(1)}, f32[10,1024]{1,0:T(8,128)S(1)}, u32[]{:S(2)}, u32[]{:S(2)}) collective-permute-start(f32[10,1024]{1,0:T(8,128)S(1)} %slice_bitcast_fusion.4), channel_id=1, source_target_pairs={{4,0},{8,4},{12,8},{16,12},{20,16},{24,20},{28,24},{5,1},{9,5},{13... | collective-permute-start | bytes 122888 | tf_op jit(solution)/shard_map/ppermute | solution.py:32
  69.9 6.3 %collective-permute-start.6 = (f32[8,1024]{1,0:T(8,128)S(1)}, f32[8,1024]{1,0:T(8,128)S(1)}, u32[]{:S(2)}, u32[]{:S(2)}) collective-permute-start(f32[8,1024]{1,0:T(8,128)S(1)} %slice_bitcast_fusion.9), channel_id=1, source_target_pairs={{0,4},{4,8},{8,12},{12,16},{16,20},{20,24},{24,28},{1,5},{5,9},{9,... | collective-permute-start | bytes 98312 | tf_op jit(solution)/shard_map/ppermute | solution.py:32
  76.5 4.4 collective-permute-start.8
  77.8 4.4 collective-permute-start.7
  115.3 6.7 %collective-permute-start.9 = (f32[10,1024]{1,0:T(8,128)S(1)}, f32[10,1024]{1,0:T(8,128)S(1)}, u32[]{:S(2)}, u32[]{:S(2)}) collective-permute-start(f32[10,1024]{1,0:T(8,128)S(1)} %slice_bitcast_fusion.3), channel_id=1, source_target_pairs={{4,0},{8,4},{12,8},{16,12},{20,16},{24,20},{28,24},{5,1},{9,5},{13... | collective-permute-start | bytes 122888 | tf_op jit(solution)/shard_map/ppermute | solution.py:32
  125.0 6.1 collective-permute-start.10
  131.4 4.8 collective-permute-start.12
  132.7 4.4 collective-permute-start.11
  142.6 17.1 %copy-start.66 = (f32[24,512]{1,0:T(8,128)S(1)}, f32[24,512]{1,0:T(8,128)}, u32[]{:S(2)}) copy-start(f32[24,512]{1,0:T(8,128)} %get-tuple-element.120) | copy-start | bytes 147460
  142.6 17.1 %copy-start.77 = (f32[24,512]{1,0:T(8,128)S(1)}, f32[24,512]{1,0:T(8,128)}, u32[]{:S(2)}) copy-start(f32[24,512]{1,0:T(8,128)} %copy-done.76) | copy-start | bytes 147460
  168.3 7.1 %collective-permute-start.13 = (f32[10,1024]{1,0:T(8,128)S(1)}, f32[10,1024]{1,0:T(8,128)S(1)}, u32[]{:S(2)}, u32[]{:S(2)}) collective-permute-start(f32[10,1024]{1,0:T(8,128)S(1)} %slice_bitcast_fusion.2), channel_id=1, source_target_pairs={{4,0},{8,4},{12,8},{16,12},{20,16},{24,20},{28,24},{5,1},{9,5},{13... | collective-permute-start | bytes 122888 | tf_op jit(solution)/shard_map/ppermute | solution.py:32
  178.4 6.1 collective-permute-start.14
  184.8 4.5 collective-permute-start.16
  186.1 4.4 collective-permute-start.15
  224.9 7.1 %collective-permute-start.17 = (f32[10,1024]{1,0:T(8,128)S(1)}, f32[10,1024]{1,0:T(8,128)S(1)}, u32[]{:S(2)}, u32[]{:S(2)}) collective-permute-start(f32[10,1024]{1,0:T(8,128)S(1)} %slice_bitcast_fusion.1), channel_id=1, source_target_pairs={{4,0},{8,4},{12,8},{16,12},{20,16},{24,20},{28,24},{5,1},{9,5},{13... | collective-permute-start | bytes 122888 | tf_op jit(solution)/shard_map/ppermute | solution.py:32
  234.9 13.2 %copy-start.19 = (f32[24,8,1024]{2,1,0:T(8,128)}, f32[24,8,1024]{2,1,0:T(8,128)S(1)}, u32[]{:S(2)}) copy-start(f32[24,8,1024]{2,1,0:T(8,128)S(1)} %get-tuple-element.64) | copy-start | bytes 2359300
  234.9 6.4 %collective-permute-start.18 = (f32[8,1024]{1,0:T(8,128)S(1)}, f32[8,1024]{1,0:T(8,128)S(1)}, u32[]{:S(2)}, u32[]{:S(2)}) collective-permute-start(f32[8,1024]{1,0:T(8,128)S(1)} %slice_bitcast_fusion.6), channel_id=1, source_target_pairs={{0,4},{4,8},{8,12},{12,16},{16,20},{20,24},{24,28},{1,5},{5,9},{9,... | collective-permute-start | bytes 98312 | tf_op jit(solution)/shard_map/ppermute | solution.py:32
  241.6 4.6 collective-permute-start.20
  242.9 4.4 collective-permute-start.19
  252.8 17.1 %copy-start.67 = (f32[24,512]{1,0:T(8,128)S(1)}, f32[24,512]{1,0:T(8,128)}, u32[]{:S(2)}) copy-start(f32[24,512]{1,0:T(8,128)} %get-tuple-element.120) | copy-start | bytes 147460
  252.8 17.1 %copy-start.72 = (f32[24,512]{1,0:T(8,128)S(1)}, f32[24,512]{1,0:T(8,128)}, u32[]{:S(2)}) copy-start(f32[24,512]{1,0:T(8,128)} %get-tuple-element.122) | copy-start | bytes 147460
  252.8 17.1 %copy-start.79 = (f32[24,512]{1,0:T(8,128)S(1)}, f32[24,512]{1,0:T(8,128)}, u32[]{:S(2)}) copy-start(f32[24,512]{1,0:T(8,128)} %copy-done.78) | copy-start | bytes 147460
  278.4 6.8 %collective-permute-start.21 = (f32[10,1024]{1,0:T(8,128)S(1)}, f32[10,1024]{1,0:T(8,128)S(1)}, u32[]{:S(2)}, u32[]{:S(2)}) collective-permute-start(f32[10,1024]{1,0:T(8,128)S(1)} %slice_bitcast_fusion), channel_id=1, source_target_pairs={{4,0},{8,4},{12,8},{16,12},{20,16},{24,20},{28,24},{5,1},{9,5},{13... | collective-permute-start | bytes 122888 | tf_op jit(solution)/shard_map/ppermute | solution.py:32
  289.7 6.1 collective-permute-start.22
  296.0 5.1 collective-permute-start.24
  297.3 4.7 collective-permute-start.23
  333.9 7.2 %collective-permute-start.25 = (f32[10,1024]{1,0:T(8,128)S(1)}, f32[10,1024]{1,0:T(8,128)S(1)}, u32[]{:S(2)}, u32[]{:S(2)}) collective-permute-start(f32[10,1024]{1,0:T(8,128)S(1)} %bitcast.237), channel_id=1, source_target_pairs={{4,0},{8,4},{12,8},{16,12},{20,16},{24,20},{28,24},{5,1},{9,5},{13... | collective-permute-start | bytes 122888 | tf_op jit(solution)/shard_map/ppermute | solution.py:32
  343.7 6.1 collective-permute-start.26
  350.0 4.6 collective-permute-start.28
  351.3 4.7 collective-permute-start.27
  359.0 17.6 %copy-start.69 = (f32[24,512]{1,0:T(8,128)S(1)}, f32[24,512]{1,0:T(8,128)}, u32[]{:S(2)}) copy-start(f32[24,512]{1,0:T(8,128)} %copy-done.68) | copy-start | bytes 147460
  359.0 17.6 %copy-start.73 = (f32[24,512]{1,0:T(8,128)S(1)}, f32[24,512]{1,0:T(8,128)}, u32[]{:S(2)}) copy-start(f32[24,512]{1,0:T(8,128)} %get-tuple-element.122) | copy-start | bytes 147460
  359.0 17.6 %copy-start.74 = (f32[24,512]{1,0:T(8,128)S(1)}, f32[24,512]{1,0:T(8,128)}, u32[]{:S(2)}) copy-start(f32[24,512]{1,0:T(8,128)} %get-tuple-element.126) | copy-start | bytes 147460
  359.0 17.6 %copy-start.81 = (f32[24,512]{1,0:T(8,128)S(1)}, f32[24,512]{1,0:T(8,128)}, u32[]{:S(2)}) copy-start(f32[24,512]{1,0:T(8,128)} %copy-done.80) | copy-start | bytes 147460
  359.1 18.3 %copy-start.93 = (f32[10]{0:T(128)S(1)}, f32[10]{0:T(128)}, u32[]{:S(2)}) copy-start(f32[10]{0:T(128)} %copy-done.88) | copy-start | bytes 124
  385.5 7.2 %collective-permute-start.29 = (f32[10,1024]{1,0:T(8,128)S(1)}, f32[10,1024]{1,0:T(8,128)S(1)}, u32[]{:S(2)}, u32[]{:S(2)}) collective-permute-start(f32[10,1024]{1,0:T(8,128)S(1)} %bitcast.239), channel_id=1, source_target_pairs={{4,0},{8,4},{12,8},{16,12},{20,16},{24,20},{28,24},{5,1},{9,5},{13... | collective-permute-start | bytes 122888 | tf_op jit(solution)/shard_map/ppermute | solution.py:32
  395.0 6.1 collective-permute-start.30
  401.3 4.6 collective-permute-start.32
  402.6 4.7 collective-permute-start.31
  439.3 7.1 %collective-permute-start.33 = (f32[10,1024]{1,0:T(8,128)S(1)}, f32[10,1024]{1,0:T(8,128)S(1)}, u32[]{:S(2)}, u32[]{:S(2)}) collective-permute-start(f32[10,1024]{1,0:T(8,128)S(1)} %bitcast.241), channel_id=1, source_target_pairs={{4,0},{8,4},{12,8},{16,12},{20,16},{24,20},{28,24},{5,1},{9,5},{13... | collective-permute-start | bytes 122888 | tf_op jit(solution)/shard_map/ppermute | solution.py:32
  446.5 17.4 %slice-start.16 = ((s8[8388608]{0:T(1024)(128)(4,1)}), s8[4194304]{0:T(1024)(128)(4,1)S(1)}, s32[]{:S(2)}) async-start(s8[8388608]{0:T(1024)(128)(4,1)} %bitcast.222), calls=%async_computation.16 | async-start | bytes 8388608
  448.6 13.0 %copy-start.4 = (f32[24,8,1024]{2,0,1:T(8,128)}, f32[24,8,1024]{2,0,1:T(8,128)S(1)}, u32[]{:S(2)}) copy-start(f32[24,8,1024]{2,0,1:T(8,128)S(1)} %get-tuple-element.55) | copy-start | bytes 2359300
  448.6 6.1 collective-permute-start.34
  455.0 4.6 collective-permute-start.36
  456.5 4.5 collective-permute-start.35
  464.0 17.5 %copy-start.71 = (f32[24,512]{1,0:T(8,128)S(1)}, f32[24,512]{1,0:T(8,128)}, u32[]{:S(2)}) copy-start(f32[24,512]{1,0:T(8,128)} %copy-done.70) | copy-start | bytes 147460
  464.0 17.5 %copy-start.75 = (f32[24,512]{1,0:T(8,128)S(1)}, f32[24,512]{1,0:T(8,128)}, u32[]{:S(2)}) copy-start(f32[24,512]{1,0:T(8,128)} %get-tuple-element.126) | copy-start | bytes 147460
  464.0 17.5 %copy-start.83 = (f32[24,512]{1,0:T(8,128)S(1)}, f32[24,512]{1,0:T(8,128)}, u32[]{:S(2)}) copy-start(f32[24,512]{1,0:T(8,128)} %copy-done.82) | copy-start | bytes 147460
  464.0 17.5 %copy-start.86 = (f32[24,512]{1,0:T(8,128)S(1)}, f32[24,512]{1,0:T(8,128)}, u32[]{:S(2)}) copy-start(f32[24,512]{1,0:T(8,128)} %get-tuple-element.132) | copy-start | bytes 147460
  464.0 18.1 %copy-start.94 = (f32[10]{0:T(128)S(1)}, f32[10]{0:T(128)}, u32[]{:S(2)}) copy-start(f32[10]{0:T(128)} %copy-done.88) | copy-start | bytes 124
  490.2 7.2 %collective-permute-start.37 = (f32[10,1024]{1,0:T(8,128)S(1)}, f32[10,1024]{1,0:T(8,128)S(1)}, u32[]{:S(2)}, u32[]{:S(2)}) collective-permute-start(f32[10,1024]{1,0:T(8,128)S(1)} %bitcast.243), channel_id=1, source_target_pairs={{4,0},{8,4},{12,8},{16,12},{20,16},{24,20},{28,24},{5,1},{9,5},{13... | collective-permute-start | bytes 122888 | tf_op jit(solution)/shard_map/ppermute | solution.py:32
  497.6 17.4 %slice-start.18 = ((s8[8388608]{0:T(1024)(128)(4,1)}), s8[4194304]{0:T(1024)(128)(4,1)S(1)}, s32[]{:S(2)}) async-start(s8[8388608]{0:T(1024)(128)(4,1)} %bitcast.224), calls=%async_computation.18 | async-start | bytes 8388608
  499.7 6.1 collective-permute-start.38
  506.0 4.6 collective-permute-start.40
  507.6 4.5 collective-permute-start.39
  516.9 20.8 %copy-start.95 = (f32[10]{0:T(128)S(1)}, f32[10]{0:T(128)}, u32[]{:S(2)}) copy-start(f32[10]{0:T(128)} %copy-done.88) | copy-start | bytes 124
  546.2 8.5 %collective-permute-start.41 = (f32[10,1024]{1,0:T(8,128)S(1)}, f32[10,1024]{1,0:T(8,128)}, u32[]{:S(2)}, u32[]{:S(2)}) collective-permute-start(f32[10,1024]{1,0:T(8,128)S(1)} %bitcast.236), channel_id=1, source_target_pairs={{4,0},{8,4},{12,8},{16,12},{20,16},{24,20},{28,24},{5,1},{9,5},{13... | collective-permute-start | bytes 122888 | tf_op jit(solution)/shard_map/ppermute | solution.py:32
  (94 other events, 475.5 us)
where the time goes:
time: 635 us; the launch traced here: 625 us
  blocking collectives  208 us (33%)
  starting transfers between devices  111 us (17%)
  matrix products  104 us (16%)
  other arithmetic  68.2 us (11%)
  waiting for transfers between devices  68.1 us (11%)
  local copies, waits for them, and re-layouts  42.1 us (7%)
  between operations  23.2 us (4%)
    psum x10, blocking collectives, local(): pulled = lax.psum(partial_pull, 'state')  163 us
    dot_general x10, matrix products, apply_rows(): lax.dot_general(inputs_low, matrix, (((1,), (1,)), ((), ())), preferred_e...  73.3 us
    ppermute x20, starting transfers between devices, passed_along(): lax.ppermute(value, axis, [(source, source + steps) for source in range(l...  59.4 us
    ppermute x20, waiting for transfers between devices, passed_along(): lax.ppermute(value, axis, [(source, source + steps) for source in range(l...  57.1 us
    psum x1, blocking collectives, local(): totals = lax.psum((primal_square, gap_square), ('section', 'state'))  44.8 us
    ppermute x11, starting transfers between devices, with_halo(): lax.ppermute(lax.slice_in_dim(block, block.shape[dim] - width, None, axis...  36.6 us
    unnamed x245, local copies, waits for them, and re-layouts  26.7 us
    reduce_sum x10, other arithmetic, local(): primal_square = jnp.sum(primal * primal)  23.2 us
  transfers between devices with their start and end apart: 42, of which 26 were waited for; matrix products, arithmetic and copies ran while one was open for 5% of the time, Pallas kernels for 0%

commit v1 on v0

v1 whole, which is shorter than its diff:
```python
import functools

import jax
import jax.numpy as jnp
from jax import lax
from jax.experimental import pallas as pl
from jax.experimental.pallas import tpu as pltpu
from jax.sharding import PartitionSpec as P

GX = 32
GY = 32
GZ = 32
ITERS = 10
LANES = 128

diffusion = 0.15
epsilon = 1e-06

VMEM_LIMIT = 48 * 1024 * 1024


def xor_pairs(count, mask):
    return [(i, i ^ mask) for i in range(count)]


def odd_masks(count):
    return sorted({i ^ (i + 1) for i in range(1, count - 1, 2)})


def swapped(value, axis, mask):
    return lax.ppermute(value, axis, xor_pairs(lax.axis_size(axis), mask))


def across_odd(values, axis):
    count = lax.axis_size(axis)
    masks = odd_masks(count)
    seat = lax.axis_index(axis)
    result = jnp.zeros_like(values)
    for mask in masks:
        got = swapped(values, axis, mask)
        lower = seat ^ mask
        near = (seat % 2 == 1) & (lower == seat + 1) | (seat % 2 == 0) & (lower + 1 == seat)
        result = jnp.where(near, got, result)
    return result


def bulk_across_odd(value, axis):
    count = lax.axis_size(axis)
    pairs = []
    for i in range(1, count - 1, 2):
        pairs += [(i, i + 1), (i + 1, i)]
    if not pairs:
        return jnp.zeros_like(value)
    return lax.ppermute(value, axis, pairs)


def lane_masks(rows):
    lane = lax.broadcasted_iota(jnp.int32, (rows, LANES), 1)
    return lane < GZ, lane >= LANES - GZ, lane % GZ == 0, lane % GZ == GZ - 1


def stencil_columns(read, columns, masks):
    first_y, last_y, first_z, last_z = masks
    centre = [read(0, j) for j in range(columns)]
    up = [pltpu.roll(c, GZ, 1) for c in centre]
    down = [pltpu.roll(c, LANES - GZ, 1) for c in centre]
    out = []
    for j in range(columns):
        above = up[j - 1] if j > 0 else 0.0
        below = down[j + 1] if j < columns - 1 else 0.0
        total = jnp.where(first_y, above, up[j]) + jnp.where(last_y, below, down[j])
        total += jnp.where(first_z, 0.0, pltpu.roll(centre[j], 1, 1))
        total += jnp.where(last_z, 0.0, pltpu.roll(centre[j], LANES - 1, 1))
        total += read(-1, j) + read(1, j)
        out.append((1.0 - 6.0 * diffusion) * centre[j] + diffusion * total)
    return out


def column(j):
    return slice(j * LANES, (j + 1) * LANES)


def inputs_step(parts, boxed_ref, scaled_ref, bound_ref, kkt_ref, penalty, own):
    sums = [p[...].astype(jnp.float32) for p in parts]
    while len(sums) > 1:
        sums = [sums[i] + sums[i + 1] for i in range(0, len(sums), 2)]
    boxed = boxed_ref[...]
    scaled = scaled_ref[...]
    rhs = sums[0] + penalty * (boxed - scaled)
    inputs = jnp.dot(
        rhs, kkt_ref[...], precision=lax.Precision.HIGHEST, preferred_element_type=jnp.float32
    )
    bound = bound_ref[...]
    boxed_new = jnp.clip(inputs + scaled, -bound, bound)
    gap = inputs - boxed_new
    square = gap * gap
    total = square[0:8]
    for i in range(8, own, 8):
        total = total + square[i : i + 8]
    return inputs, boxed_new, scaled + gap, total


def drive(inputs_low, block):
    return lax.dot_general(
        inputs_low, block, (((1,), (1,)), ((), ())), preferred_element_type=jnp.float32
    )


def defect_planes(
    flags, inputs_low, matrix_ref, near_ref, far_ref, target_ref, near_rim, far_rim, defect_ref
):
    planes = target_ref.shape[0]

    def own_plane(p, _):
        defect_ref[p + 2] = target_ref[p] - drive(inputs_low, matrix_ref[p])
        return 0

    lax.fori_loop(0, planes, own_plane, 0)
    even = flags[0]
    keep = flags[1].astype(jnp.float32)
    near_base = even * (planes + 2)
    far_base = (1 - even) * (planes + 2)
    for i in range(2):
        defect_ref[near_base + i] = near_rim[i].astype(jnp.float32) - drive(inputs_low, near_ref[i])
        defect_ref[far_base + i] = keep * (
            far_rim[i].astype(jnp.float32) - drive(inputs_low, far_ref[i])
        )


def step_kernel(groups, own, halo, penalty, with_extra, *refs):
    refs = list(refs)
    flags = refs.pop(0)
    parts = [refs.pop(0) for _ in range(groups)]
    boxed_ref, scaled_ref, bound_ref, kkt_ref = [refs.pop(0) for _ in range(4)]
    matrix_ref, near_ref, far_ref = [refs.pop(0) for _ in range(3)]
    target_ref, near_rim, far_rim = [refs.pop(0) for _ in range(3)]
    states_ref, duals_ref, inverse_ref, goal_ref = [refs.pop(0) for _ in range(4)]
    extra_ref = refs.pop(0) if with_extra else None
    boxed_out, scaled_out, states_out, duals_out, target_out = [refs.pop(0) for _ in range(5)]
    part_out, near_out, far_out, primal_out, gap_out = [refs.pop(0) for _ in range(5)]
    defect_ref, low_ref = refs

    planes, rows, plane_size = target_ref.shape
    columns = plane_size // LANES
    inputs, boxed_new, scaled_new, gap_total = inputs_step(
        parts, boxed_ref, scaled_ref, bound_ref, kkt_ref, penalty, own
    )
    boxed_out[...] = boxed_new
    scaled_out[...] = scaled_new
    gap_out[...] = gap_total
    inputs_low = inputs.astype(jnp.bfloat16)
    defect_planes(
        flags, inputs_low, matrix_ref, near_ref, far_ref, target_ref, near_rim, far_rim, defect_ref
    )
    masks = lane_masks(rows)

    def new_states(q, keep_duals, total):
        def read(offset, j):
            return defect_ref[q + 1 + offset, :, column(j)]

        spread = stencil_columns(read, columns, masks)
        for j in range(columns):
            ahead = pltpu.roll(spread[j], rows - 1, 0)
            defect = defect_ref[q + 1, :, column(j)]
            old = states_ref[q, :, column(j)]
            new = goal_ref[q, :, column(j)] + inverse_ref[q, :, column(j)] * (
                (old - defect) + ahead + old
            )
            states_out[q, :, column(j)] = new
            if keep_duals:
                dual = (new - old) + defect
                primal = dual - duals_ref[q - 1, :, column(j)]
                duals_out[q - 1, :, column(j)] = dual
                square = primal * primal
                for i in range(0, own, 8):
                    total = total + square[i : i + 8]
        return total

    zero = jnp.zeros((8, LANES), jnp.float32)
    new_states(0, False, zero)
    new_states(planes + 1, False, zero)
    primal_out[...] = lax.fori_loop(
        1, planes + 1, lambda q, total: new_states(q, True, total), zero
    )

    row = lax.broadcasted_iota(jnp.int32, (rows, LANES), 0)
    live = (row < own) | (row < own + halo) & (flags[3] == 0) | (row >= own + halo) & (flags[2] == 0)

    def new_target(p, total):
        def read(offset, j):
            return states_out[p + 1 + offset, :, column(j)]

        spread = stencil_columns(read, columns, masks)
        for j in range(columns):
            moved = pltpu.roll(spread[j], 1, 0)
            if with_extra:
                moved = jnp.where(row == own + halo, extra_ref[p, 0:1, column(j)], moved)
            new = (states_out[p + 1, :, column(j)] - moved) + duals_out[p, :, column(j)]
            new = jnp.where(live, new, 0.0)
            target_out[p, :, column(j)] = new
            low_ref[p, :, column(j)] = new.astype(jnp.bfloat16)
        return total + jnp.dot(low_ref[p], matrix_ref[p], preferred_element_type=jnp.float32)

    width = matrix_ref.shape[2]
    part = lax.fori_loop(0, planes, new_target, jnp.zeros((rows, width), jnp.float32))
    part_out[...] = part.astype(jnp.bfloat16)
    near_base = flags[0] * (planes - 2)
    far_base = (1 - flags[0]) * (planes - 2)
    for i in range(2):
        near_out[i] = low_ref[near_base + i]
        far_out[i] = low_ref[far_base + i]


def last_inputs_kernel(groups, own, penalty, *refs):
    refs = list(refs)
    flags = refs.pop(0)
    parts = [refs.pop(0) for _ in range(groups)]
    boxed_ref, scaled_ref, bound_ref, kkt_ref = [refs.pop(0) for _ in range(4)]
    matrix_ref, near_ref, far_ref = [refs.pop(0) for _ in range(3)]
    target_ref, near_rim, far_rim = [refs.pop(0) for _ in range(3)]
    boxed_out, gap_out, defect_out, first_out = refs
    inputs, boxed_new, _, gap_total = inputs_step(
        parts, boxed_ref, scaled_ref, bound_ref, kkt_ref, penalty, own
    )
    boxed_out[...] = boxed_new
    gap_out[...] = gap_total
    defect_planes(
        flags,
        inputs.astype(jnp.bfloat16),
        matrix_ref,
        near_ref,
        far_ref,
        target_ref,
        near_rim,
        far_rim,
        defect_out,
    )
    first_out[...] = defect_out[:, 0:8, :]


def last_states_kernel(
    own, defect_ref, following_ref, states_ref, duals_ref, inverse_ref, goal_ref, *outs
):
    states_out, duals_out, primal_out = outs
    planes = states_out.shape[0]
    columns = states_out.shape[2] // LANES
    masks = lane_masks(own)
    last = lax.broadcasted_iota(jnp.int32, (own, LANES), 0) == own - 1

    def body(p, total):
        def read(offset, j):
            own_rows = defect_ref[p + 2 + offset, 0:own, column(j)]
            after = following_ref[p + 2 + offset, 0:1, column(j)]
            return jnp.where(last, after, pltpu.roll(own_rows, own - 1, 0))

        spread = stencil_columns(read, columns, masks)
        for j in range(columns):
            defect = defect_ref[p + 2, 0:own, column(j)]
            old = states_ref[p + 1, 0:own, column(j)]
            new = goal_ref[p + 1, 0:own, column(j)] + inverse_ref[p + 1, 0:own, column(j)] * (
                (old - defect) + spread[j] + old
            )
            dual = (new - old) + defect
            primal = dual - duals_ref[p, 0:own, column(j)]
            states_out[p, :, column(j)] = new
            duals_out[p, :, column(j)] = dual
            square = primal * primal
            for i in range(0, own, 8):
                total = total + square[i : i + 8]
        return total

    primal_out[...] = lax.fori_loop(0, planes, body, jnp.zeros((8, LANES), jnp.float32))


def in_vmem(count):
    return [pl.BlockSpec(memory_space=pltpu.VMEM)] * count


def call(kernel, flags, operands, outs, scratch=(), flops=0):
    specs = in_vmem(len(operands))
    if flags is not None:
        specs = [pl.BlockSpec(memory_space=pltpu.SMEM)] + specs
        operands = (flags, *operands)
    return pl.pallas_call(
        kernel,
        out_shape=outs,
        in_specs=specs,
        out_specs=tuple(in_vmem(len(outs))),
        scratch_shapes=list(scratch),
        compiler_params=pltpu.CompilerParams(vmem_limit_bytes=VMEM_LIMIT),
        cost_estimate=pl.CostEstimate(flops=flops, bytes_accessed=30_000_000, transcendentals=0),
    )(*operands)


def all_sum(value, axis):
    mask = 1
    while mask < lax.axis_size(axis):
        value = value + swapped(value, axis, mask)
        mask *= 2
    return value


def local(initial_state, state_ref, state_weight, input_matrix, kkt_inverse, input_bound):
    own, planes, plane_size = state_ref.shape
    width = input_matrix.shape[2]
    halo = ITERS - 2
    rows = own + 2 * halo
    assert own > halo and own % 8 == 0 and halo % 8 == 0 and plane_size == GY * GZ
    penalty = float(GX * GY * GZ) / width
    groups = lax.axis_size("state")
    sections = lax.axis_size("section")
    seat = lax.axis_index("state")
    section = lax.axis_index("section")
    even = seat % 2 == 0
    even_section = section % 2 == 0
    is_first = section == 0
    is_last = section == sections - 1
    far_lives = jnp.logical_not((seat == 0) | (seat == groups - 1) & (groups % 2 == 0))
    flags = jnp.stack(
        [even.astype(jnp.int32), far_lives.astype(jnp.int32), is_first.astype(jnp.int32), is_last.astype(jnp.int32)]
    )

    top = input_matrix[planes - 2 :]
    bottom = input_matrix[:2]
    near_matrix = swapped(jnp.where(even, top, bottom), "state", 1)
    far_matrix = across_odd(jnp.where(even, bottom, top), "state")

    inverse = 1.0 / (state_weight + 2.0)
    goal = state_weight * state_ref * inverse
    both = jnp.stack([goal, inverse]).transpose(0, 2, 1, 3)
    to_next = both[:, :, own - halo - 1 :]
    to_previous = both[:, :, : halo + 1]
    paired = swapped(jnp.where(even_section, to_next, to_previous).astype(jnp.bfloat16), "section", 1)
    other = bulk_across_odd(
        jnp.where(even_section, to_previous, to_next).astype(jnp.bfloat16), "section"
    )
    paired = paired.astype(jnp.float32)
    other = other.astype(jnp.float32)
    from_next = jnp.where(even_section, paired, other)
    from_previous = jnp.where(even_section, other, paired)
    pinned = jnp.concatenate(
        [jnp.zeros((planes, halo, plane_size), jnp.float32), initial_state[:, None]], 1
    )
    pinned = jnp.stack([pinned, jnp.zeros_like(pinned)])
    from_previous = jnp.where(is_first, pinned, from_previous)
    wide = jnp.concatenate(
        [both, from_next[:, :, :halo], from_previous[:, :, 1:], from_previous[:, :, :1]], 2
    )
    near_plane = swapped(jnp.where(even, wide[:, planes - 1], wide[:, 0]), "state", 1)
    far_plane = across_odd(jnp.where(even, wide[:, 0], wide[:, planes - 1]), "state")
    far_plane = jnp.where(far_lives, far_plane, 0.0)
    low_plane = jnp.where(even, far_plane, near_plane)
    high_plane = jnp.where(even, near_plane, far_plane)
    wide = jnp.concatenate([low_plane[:, None], wide, high_plane[:, None]], 1)
    goal = wide[0, :, :rows]
    inverse = wide[1, :, :rows]
    extra = wide[0, :, rows]

    near_state = swapped(jnp.where(even, initial_state[planes - 1], initial_state[0]), "state", 1)
    far_state = across_odd(jnp.where(even, initial_state[0], initial_state[planes - 1]), "state")
    far_state = jnp.where(far_lives, far_state, 0.0)
    low_state = jnp.where(even, far_state, near_state)
    high_state = jnp.where(even, near_state, far_state)

    def stencil(padded):
        centre = padded[1:-1]
        grid = centre.reshape(-1, GY, GZ)
        total = padded[2:] + padded[:-2]
        in_y = jnp.pad(grid, ((0, 0), (1, 1), (0, 0)))
        in_z = jnp.pad(grid, ((0, 0), (0, 0), (1, 1)))
        total += (in_y[:, 2:] + in_y[:, :-2] + in_z[:, :, 2:] + in_z[:, :, :-2]).reshape(centre.shape)
        return (1.0 - 6.0 * diffusion) * centre + diffusion * total

    moved = stencil(jnp.concatenate([low_state[None], initial_state, high_state[None]]))
    extra_moved = jnp.broadcast_to(stencil(extra)[:, None], (planes, 8, plane_size))
    first = jnp.where(is_first, -moved, 0.0)
    target = jnp.concatenate(
        [first[:, None], jnp.zeros((planes, rows - 1, plane_size), jnp.float32)], 1
    )
    first_low = first.astype(jnp.bfloat16)
    first_part = jnp.dot(
        jnp.broadcast_to(first_low.reshape(1, -1), (8, planes * plane_size)),
        input_matrix.reshape(planes * plane_size, width),
        preferred_element_type=jnp.float32,
    )
    part = jnp.concatenate(
        [first_part[:1], jnp.zeros((rows - 1, width), jnp.float32)], 0
    ).astype(jnp.bfloat16)
    rims = target.astype(jnp.bfloat16)
    near_rim = jnp.where(even, rims[planes - 2 :], rims[:2])
    far_rim = jnp.where(even, rims[:2], rims[planes - 2 :])

    states = jnp.zeros((planes + 2, rows, plane_size), jnp.float32)
    duals = jnp.zeros((planes, rows, plane_size), jnp.float32)
    boxed = jnp.zeros((rows, width), jnp.float32)
    scaled = jnp.zeros((rows, width), jnp.float32)
    bound = input_bound.reshape(1, width)

    f32 = jnp.float32
    shape = jax.ShapeDtypeStruct
    vector = shape((8, LANES), f32)
    small = shape((rows, width), f32)
    rim_shape = shape((2, rows, plane_size), jnp.bfloat16)
    flops = 4 * rows * width * planes * plane_size
    primals = []
    gaps = []
    for iteration in range(ITERS):
        parts = [part] + [swapped(part, "state", mask) for mask in range(1, groups)]
        near_in = swapped(near_rim, "state", 1)
        far_in = across_odd(far_rim, "state")
        head = (*parts, boxed, scaled, bound, kkt_inverse, input_matrix, near_matrix, far_matrix)
        head = (*head, target, near_in, far_in)
        if iteration < ITERS - 1:
            with_extra = iteration == 0
            tail = (states, duals, inverse, goal) + ((extra_moved,) if with_extra else ())
            outs = (
                small,
                small,
                shape(states.shape, f32),
                shape(duals.shape, f32),
                shape(target.shape, f32),
                shape((rows, width), jnp.bfloat16),
                rim_shape,
                rim_shape,
                vector,
                shape((8, width), f32),
            )
            boxed, scaled, states, duals, target, part, near_rim, far_rim, primal, gap = call(
                functools.partial(step_kernel, groups, own, halo, penalty, with_extra),
                flags,
                head + tail,
                outs,
                [
                    pltpu.VMEM((planes + 4, rows, plane_size), f32),
                    pltpu.VMEM((planes, rows, plane_size), jnp.bfloat16),
                ],
                flops,
            )
        else:
            defect_shape = (planes + 4, rows, plane_size)
            boxed, gap, defect, edge = call(
                functools.partial(last_inputs_kernel, groups, own, penalty),
                flags,
                head,
                (
                    small,
                    shape((8, width), f32),
                    shape(defect_shape, f32),
                    shape((planes + 4, 8, plane_size), f32),
                ),
                (),
                flops // 2,
            )
            edge = edge[:, 0]
            following = jnp.where(
                even_section, swapped(edge, "section", 1), across_odd(edge, "section")
            )
            following = jnp.where(is_last, 0.0, following)
            following = jnp.broadcast_to(following[:, None], (planes + 4, 8, plane_size))
            own_shape = shape((planes, own, plane_size), f32)
            states, duals, primal = call(
                functools.partial(last_states_kernel, own),
                None,
                (defect, following, states, duals, inverse, goal),
                (own_shape, own_shape, vector),
                (),
                1_000_000,
            )
        primals.append(primal)
        gaps.append(gap)

    primal_square = jnp.sum(jnp.stack(primals), (1, 2))
    gap_square = jnp.sum(jnp.stack(gaps), (1, 2)) / groups
    totals = jnp.stack([primal_square, gap_square], 1)
    totals = jnp.pad(totals.reshape(1, -1), ((0, 7), (0, LANES - 2 * ITERS)))
    totals = all_sum(all_sum(totals, "state"), "section")
    totals = totals[0, : 2 * ITERS].reshape(ITERS, 2)
    total_sections = own * sections
    counts = jnp.array([total_sections * GX * GY * GZ, total_sections * width], f32)
    record = jnp.sqrt(totals / counts + epsilon)
    return (
        states.transpose(1, 0, 2),
        boxed[:own],
        duals.transpose(1, 0, 2),
        record,
    )


def solution(mesh):
    return jax.shard_map(
        local,
        mesh=mesh,
        in_specs=(
            P("state", None),
            P("section", "state", None),
            P("section", "state", None),
            P("state", None, None),
            P(),
            P(),
        ),
        out_specs=(
            P("section", "state", None),
            P("section", None),
            P("section", "state", None),
            P(),
        ),
        check_vma=False,
    )
```

time: 635 us -> 407 us (0.64)
  blocking collectives: 208 us -> 0 us
  Pallas kernels: 0 us -> 170 us
  matrix products: 104 us -> 4.6 us
  starting transfers between devices: 111 us -> 52.8 us
  other arithmetic: 68.2 us -> 19.5 us
  waiting for transfers between devices: 68.1 us -> 109 us
  between operations: 23.2 us -> 1.99 us
    psum x11 -> x0, blocking collectives: 208 us -> none  [the longest x10 163 us: local(): pulled = lax.psum(partial_pull, 'state')]
    pallas_call x0 -> x9, Pallas kernels: none -> 170 us  [call(): pl.pallas_call(kernel, out_shape=outs, in_specs=specs, out_specs=tuple(in...]
    dot_general x30 -> x1, matrix products: 104 us -> 4.6 us  [local(): jnp.dot(jnp.broadcast_to(first_low.reshape(1, -1), (8, planes * plane_siz...]
    ppermute x42 -> x66, starting transfers between devices: 111 us -> 52.8 us  [the longest x65 52.2 us: swapped(): return lax.ppermute(value, axis, xor_pairs(lax.axis_size(axis), mask))]
    ppermute x42 -> x66, waiting for transfers between devices: 68.1 us -> 109 us  [the longest x65 109 us: swapped(): return lax.ppermute(value, axis, xor_pairs(lax.axis_size(axis), mask))]
    add x20 -> x9, other arithmetic: 26.3 us -> 1.41 us  [the longest x1 1.09 us: stencil(): total = padded[2:] + padded[:-2]]
    reduce_sum x10 -> x2, other arithmetic: 23.2 us -> 0.31 us  [the longest x1 0.16 us: local(): gap_square = jnp.sum(jnp.stack(gaps), (1, 2)) / groups]
    pallas_call x0 -> x11, local copies, waits for them, and re-layouts: none -> 16.9 us  [call(): pl.pallas_call(kernel, out_shape=outs, in_specs=specs, out_specs=tuple(in...]
  transfers between devices with their start and end apart: 42 -> 66, of which waited for: 26 -> 17; matrix products, arithmetic and copies ran while one was open for 5% -> 10% of each run, Pallas kernels for 0% -> 0%
where the time goes in v1:
time: 407 us; the launch traced here: 402 us
  Pallas kernels  170 us (42%)
  waiting for transfers between devices  109 us (27%)
  starting transfers between devices  52.8 us (13%)
  local copies, waits for them, and re-layouts  44.2 us (11%)
  other arithmetic  19.5 us (5%)
  matrix products  4.6 us (1%)
    pallas_call x9, Pallas kernels, call(): pl.pallas_call(kernel, out_shape=outs, in_specs=specs, out_specs=tuple(in...  170 us
    ppermute x65, waiting for transfers between devices, swapped(): return lax.ppermute(value, axis, xor_pairs(lax.axis_size(axis), mask))  109 us
    ppermute x65, starting transfers between devices, swapped(): return lax.ppermute(value, axis, xor_pairs(lax.axis_size(axis), mask))  52.2 us
    unnamed x63, local copies, waits for them, and re-layouts  17.6 us
    pallas_call x11, local copies, waits for them, and re-layouts, call(): pl.pallas_call(kernel, out_shape=outs, in_specs=specs, out_specs=tuple(in...  16.9 us
  transfers between devices with their start and end apart: 66, of which 17 were waited for; matrix products, arithmetic and copies ran while one was open for 10% of the time, Pallas kernels for 0%

profile of v1, /device:TPU:0, one launch (start us, length us, event | category | flops | bytes accessed | tf_op | source)
XLA Modules:
  0.0 402.4 jit_solution(13039899670382122634)
XLA Ops:
  0.6 1.6 multiply_bitcast_fusion
  2.5 3.1 collective-permute-start.9
  6.2 4.5 %broadcast_select_fusion.1 = (bf16[2,1024,512]{2,1,0:T(8,128)(2,1)}, bf16[2,1024,512]{2,1,0:T(8,128)(2,1)}) fusion(pred[]{:T(512)} %eq.61, bf16[8,1024,512]{2,1,0:T(8,128)(2,1)} %refs_9_.18), kind=kLoop, calls=%fused_computation.1 | loop fusion | flops 2097152 | bytes 8388609 | tf_op jit(solution)/shard_map/jit(_where)/select_n | solution.py:326
  12.7 2.1 copy_dynamic-update-slice_fusion
  16.5 42.5 %collective-permute-done.1 = f32[1024]{0:T(1024)S(1)} collective-permute-done((f32[1024]{0:T(1024)S(1)}, f32[1024]{0:T(1024)S(1)}, u32[]{:S(2)}, u32[]{:S(2)}) %collective-permute-start.1) | collective-permute-done | bytes 4128 | tf_op jit(solution)/shard_map/ppermute | solution.py:31
  59.1 1.1 broadcast_select_fusion.13
  61.1 4.6 %fusion.14 = bf16[8,512]{1,0:T(8,128)(2,1)S(1)} fusion(bf16[8192,512]{1,0:T(8,128)(2,1)} %bitcast.115, bf16[8192]{0:T(1024)(128)(2,1)S(1)} %bitcast.119), kind=kOutput, calls=%fused_computation.53 | convolution fusion | flops 67108864 | bytes 8413184 | tf_op jit(solution)/shard_map/dot_general | solution.py:381
  65.7 1.2 concatenate.31.clone.refs_12_
  68.0 1.1 copy_dynamic-update-slice_fusion.2
  69.2 1.1 copy_dynamic-update-slice_fusion.1
  70.3 2.1 dynamic-update-slice.23
  72.5 2.1 select_bitcast_fusion.1
  77.0 9.0 %collective-permute-done.11 = f32[2,41,1024]{2,1,0:T(8,128)} collective-permute-done((f32[2,41,1024]{2,1,0:T(8,128)}, f32[2,41,1024]{2,1,0:T(8,128)}, u32[]{:S(2)}, u32[]{:S(2)}) %collective-permute-start.11) | collective-permute-done | bytes 335904 | tf_op jit(solution)/shard_map/ppermute | solution.py:31
  87.5 1.2 fusion.12
  88.7 1.1 fusion.16
  89.8 3.9 fusion
  93.7 1.4 broadcast_select_fusion.refs_11_
  95.3 1.5 broadcast_in_dim.77.refs_15_
  96.7 1.2 broadcast_in_dim.78.refs_16_
  98.0 19.2 %shard_map.102 = (f32[40,512]{1,0:T(8,128)S(1)}, f32[40,512]{1,0:T(8,128)S(1)}, f32[10,40,1024]{2,1,0:T(8,128)}, f32[8,40,1024]{2,1,0:T(8,128)S(1)}, f32[8,40,10...) custom-call(s32[4]{0:T(128)S(1)} %add_convert_fusion.refs_0_, ...), custom_call_target="tpu_custom_call" | custom-call | flops 671088640 | bytes 30000000 | tf_op jit(solution)/shard_map/pallas_call | solution.py:284
  117.1 1.1 copy-done.8
  118.2 2.4 collective-permute-start.13
  120.6 1.4 collective-permute-start.15
  123.1 4.7 %collective-permute-done.17 = bf16[2,40,1024]{2,0,1:T(2,128)(2,1)S(1)} collective-permute-done((bf16[2,40,1024]{2,0,1:T(2,128)(2,1)S(1)}, bf16[2,40,1024]{2,0,1:T(2,128)(2,1)S(1)}, u32[]{:S(2)}, u32[]{:S(2)}) %collective-permute-start.17) | collective-permute-done | bytes 163872 | tf_op jit(solution)/shard_map/ppermute | solution.py:31
  127.9 18.9 %shard_map.103 = (f32[40,512]{1,0:T(8,128)S(1)}, f32[40,512]{1,0:T(8,128)S(1)}, f32[10,40,1024]{2,1,0:T(8,128)}, f32[8,40,1024]{2,1,0:T(8,128)S(1)}, f32[8,40,10...) custom-call(s32[4]{0:T(128)S(1)} %add_convert_fusion.refs_0_, ...), custom_call_target="tpu_custom_call" | custom-call | flops 671088640 | bytes 30000000 | tf_op jit(solution)/shard_map/pallas_call | solution.py:284
  146.8 1.1 copy-done.1
  148.7 1.4 collective-permute-start.19
  150.4 1.7 collective-permute-start.22
  152.3 4.8 %collective-permute-done.22 = bf16[2,40,1024]{2,0,1:T(2,128)(2,1)S(1)} collective-permute-done((bf16[2,40,1024]{2,0,1:T(2,128)(2,1)S(1)}, bf16[2,40,1024]{2,0,1:T(2,128)(2,1)S(1)}, u32[]{:S(2)}, u32[]{:S(2)}) %collective-permute-start.22) | collective-permute-done | bytes 163872 | tf_op jit(solution)/shard_map/ppermute | solution.py:31
  157.3 18.8 %shard_map.104 = (f32[40,512]{1,0:T(8,128)S(1)}, f32[40,512]{1,0:T(8,128)S(1)}, f32[10,40,1024]{2,1,0:T(8,128)}, f32[8,40,1024]{2,1,0:T(8,128)S(1)}, f32[8,40,10...) custom-call(s32[4]{0:T(128)S(1)} %add_convert_fusion.refs_0_, ...), custom_call_target="tpu_custom_call" | custom-call | flops 671088640 | bytes 30000000 | tf_op jit(solution)/shard_map/pallas_call | solution.py:284
  177.4 1.2 collective-permute-start.24
  179.2 1.4 collective-permute-start.27
  180.6 4.9 %collective-permute-done.27 = bf16[2,40,1024]{2,0,1:T(2,128)(2,1)S(1)} collective-permute-done((bf16[2,40,1024]{2,0,1:T(2,128)(2,1)S(1)}, bf16[2,40,1024]{2,0,1:T(2,128)(2,1)S(1)}, u32[]{:S(2)}, u32[]{:S(2)}) %collective-permute-start.27) | collective-permute-done | bytes 163872 | tf_op jit(solution)/shard_map/ppermute | solution.py:31
  185.7 19.1 %shard_map.105 = (f32[40,512]{1,0:T(8,128)S(1)}, f32[40,512]{1,0:T(8,128)S(1)}, f32[10,40,1024]{2,1,0:T(8,128)}, f32[8,40,1024]{2,1,0:T(8,128)S(1)}, f32[8,40,10...) custom-call(s32[4]{0:T(128)S(1)} %add_convert_fusion.refs_0_, ...), custom_call_target="tpu_custom_call" | custom-call | flops 671088640 | bytes 30000000 | tf_op jit(solution)/shard_map/pallas_call | solution.py:284
  207.9 1.3 collective-permute-start.32
  209.2 4.7 %collective-permute-done.32 = bf16[2,40,1024]{2,0,1:T(2,128)(2,1)S(1)} collective-permute-done((bf16[2,40,1024]{2,0,1:T(2,128)(2,1)S(1)}, bf16[2,40,1024]{2,0,1:T(2,128)(2,1)S(1)}, u32[]{:S(2)}, u32[]{:S(2)}) %collective-permute-start.32) | collective-permute-done | bytes 163872 | tf_op jit(solution)/shard_map/ppermute | solution.py:31
  214.1 18.8 %shard_map.106 = (f32[40,512]{1,0:T(8,128)S(1)}, f32[40,512]{1,0:T(8,128)S(1)}, f32[10,40,1024]{2,1,0:T(8,128)}, f32[8,40,1024]{2,1,0:T(8,128)S(1)}, f32[8,40,10...) custom-call(s32[4]{0:T(128)S(1)} %add_convert_fusion.refs_0_, ...), custom_call_target="tpu_custom_call" | custom-call | flops 671088640 | bytes 30000000 | tf_op jit(solution)/shard_map/pallas_call | solution.py:284
  236.0 1.5 collective-permute-start.37
  237.5 4.7 %collective-permute-done.37 = bf16[2,40,1024]{2,0,1:T(2,128)(2,1)S(1)} collective-permute-done((bf16[2,40,1024]{2,0,1:T(2,128)(2,1)S(1)}, bf16[2,40,1024]{2,0,1:T(2,128)(2,1)S(1)}, u32[]{:S(2)}, u32[]{:S(2)}) %collective-permute-start.37) | collective-permute-done | bytes 163872 | tf_op jit(solution)/shard_map/ppermute | solution.py:31
  242.4 18.9 %shard_map.107 = (f32[40,512]{1,0:T(8,128)S(1)}, f32[40,512]{1,0:T(8,128)S(1)}, f32[10,40,1024]{2,1,0:T(8,128)}, f32[8,40,1024]{2,1,0:T(8,128)S(1)}, f32[8,40,10...) custom-call(s32[4]{0:T(128)S(1)} %add_convert_fusion.refs_0_, ...), custom_call_target="tpu_custom_call" | custom-call | flops 671088640 | bytes 30000000 | tf_op jit(solution)/shard_map/pallas_call | solution.py:284
  264.4 1.5 collective-permute-start.42
  265.8 4.7 %collective-permute-done.42 = bf16[2,40,1024]{2,0,1:T(2,128)(2,1)S(1)} collective-permute-done((bf16[2,40,1024]{2,0,1:T(2,128)(2,1)S(1)}, bf16[2,40,1024]{2,0,1:T(2,128)(2,1)S(1)}, u32[]{:S(2)}, u32[]{:S(2)}) %collective-permute-start.42) | collective-permute-done | bytes 163872 | tf_op jit(solution)/shard_map/ppermute | solution.py:31
  270.8 18.8 %shard_map.108 = (f32[40,512]{1,0:T(8,128)S(1)}, f32[40,512]{1,0:T(8,128)S(1)}, f32[10,40,1024]{2,1,0:T(8,128)}, f32[8,40,1024]{2,1,0:T(8,128)S(1)}, f32[8,40,10...) custom-call(s32[4]{0:T(128)S(1)} %add_convert_fusion.refs_0_, ...), custom_call_target="tpu_custom_call" | custom-call | flops 671088640 | bytes 30000000 | tf_op jit(solution)/shard_map/pallas_call | solution.py:284
  292.7 1.5 collective-permute-start.47
  294.1 4.7 %collective-permute-done.47 = bf16[2,40,1024]{2,0,1:T(2,128)(2,1)S(1)} collective-permute-done((bf16[2,40,1024]{2,0,1:T(2,128)(2,1)S(1)}, bf16[2,40,1024]{2,0,1:T(2,128)(2,1)S(1)}, u32[]{:S(2)}, u32[]{:S(2)}) %collective-permute-start.47) | collective-permute-done | bytes 163872 | tf_op jit(solution)/shard_map/ppermute | solution.py:31
  299.1 19.0 %shard_map.109 = (f32[40,512]{1,0:T(8,128)S(1)}, f32[40,512]{1,0:T(8,128)S(1)}, f32[10,40,1024]{2,1,0:T(8,128)}, f32[8,40,1024]{2,1,0:T(8,128)S(1)}, f32[8,40,10...) custom-call(s32[4]{0:T(128)S(1)} %add_convert_fusion.refs_0_, ...), custom_call_target="tpu_custom_call" | custom-call | flops 671088640 | bytes 30000000 | tf_op jit(solution)/shard_map/pallas_call | solution.py:284
  321.1 1.5 collective-permute-start.52
  322.6 4.7 %collective-permute-done.52 = bf16[2,40,1024]{2,0,1:T(2,128)(2,1)S(1)} collective-permute-done((bf16[2,40,1024]{2,0,1:T(2,128)(2,1)S(1)}, bf16[2,40,1024]{2,0,1:T(2,128)(2,1)S(1)}, u32[]{:S(2)}, u32[]{:S(2)}) %collective-permute-start.52) | collective-permute-done | bytes 163872 | tf_op jit(solution)/shard_map/ppermute | solution.py:31
  327.6 18.9 %shard_map.110 = (f32[40,512]{1,0:T(8,128)S(1)}, f32[40,512]{1,0:T(8,128)S(1)}, f32[10,40,1024]{2,1,0:T(8,128)}, f32[8,40,1024]{2,1,0:T(8,128)S(1)}, f32[8,40,10...) custom-call(s32[4]{0:T(128)S(1)} %add_convert_fusion.refs_0_, ...), custom_call_target="tpu_custom_call" | custom-call | flops 671088640 | bytes 30000000 | tf_op jit(solution)/shard_map/pallas_call | solution.py:284
  348.5 1.5 collective-permute-start.57
  350.0 4.7 %collective-permute-done.57 = bf16[2,40,1024]{2,0,1:T(2,128)(2,1)S(1)} collective-permute-done((bf16[2,40,1024]{2,0,1:T(2,128)(2,1)S(1)}, bf16[2,40,1024]{2,0,1:T(2,128)(2,1)S(1)}, u32[]{:S(2)}, u32[]{:S(2)}) %collective-permute-start.57) | collective-permute-done | bytes 163872 | tf_op jit(solution)/shard_map/ppermute | solution.py:31
  354.9 10.2 %shard_map.112 = (f32[10,8,512]{2,1,0:T(8,128)S(1)}, f32[12,40,1024]{2,1,0:T(8,128)}, f32[12,8,1024]{2,1,0:T(8,128)S(1)}, f32[40,512]{1,0:T(8,128)S(1)}) fusion(f32[10,8,512]{2,1,0:T(8,128)S(1)} %constant_dynamic-update-slice_fusion.11, s32[4]{0:T(128)S(1)} %add_convert_fusion.refs_0_, bf16[40,512]{1,0:T(8,128)(2,1)S(1)} %get-tuple-element.165, ...), kind=kCustom, calls=%fused_computation.65 | custom fusion | bytes 18057728 | tf_op jit(solution)/shard_map/pallas_call | solution.py:284
  365.2 4.1 %collective-permute-start.58 = (f32[12,1024]{1,0:T(8,128)S(1)}, f32[12,1024]{1,0:T(8,128)S(1)}, u32[]{:S(2)}, u32[]{:S(2)}) collective-permute-start(f32[12,1024]{1,0:T(8,128)S(1)} %bitcast.120), channel_id=1, source_target_pairs={{0,4},{4,0},{8,12},{12,8},{16,20},{20,16},{24,28},{28,24},{1,5},{5... | collective-permute-start | bytes 147464 | tf_op jit(solution)/shard_map/ppermute | solution.py:31
  369.2 2.4 collective-permute-start.59
  371.6 1.6 collective-permute-start.60
  373.4 3.4 collective-permute-done.59
  377.7 5.2 %shard_map.111 = (f32[10,8,128]{2,1,0:T(8,128)S(1)}, f32[8,24,1024]{2,1,0:T(8,128)}, f32[8,24,1024]{2,1,0:T(8,128)}) fusion(f32[10,8,128]{2,1,0:T(8,128)S(1)} %constant_dynamic-update-slice_fusion.1, f32[12,40,1024]{2,1,0:T(8,128)} %get-tuple-element.214, f32[12,8,1024]{2,1,0:T(8,128)S(1)} %broadcast_in_dim.85, f32[10,40,1024]{2,1,0:T(8,128)} %get-tuple-element.173, ...), kind=kCustom, calls=%fused_computation.55 | custom fusion | bytes 10162176 | tf_op jit(solution)/shard_map/pallas_call | solution.py:284
  383.4 1.2 collective-permute-done.61
  385.5 2.6 collective-permute-done.62
  388.5 3.2 collective-permute-done.63
  391.8 3.6 collective-permute-done.64
  395.4 1.4 collective-permute-start.65
  397.3 2.5 copy.72
  399.8 1.3 copy.73
  (231 shorter events, 38.3 us)
Async XLA Ops:
  2.5 64.4 %collective-permute-start.9 = (bf16[2,8,9,1024]{3,1,2,0:T(8,128)(2,1)S(1)}, bf16[2,8,9,1024]{3,1,2,0:T(8,128)(2,1)S(1)}, u32[]{:S(2)}, u32[]{:S(2)}) collective-permute-start(bf16[2,8,9,1024]{3,1,2,0:T(8,128)(2,1)S(1)} %get-tuple-element.226), channel_id=1, source_target_pairs={{0,4},{4,0},{8,12},{12,8},{16,20},{20,16},{24,28},{28,24},{1,5},{5... | collective-permute-start | bytes 884744 | tf_op jit(solution)/shard_map/ppermute | solution.py:31
  5.5 62.1 %collective-permute-start.10 = (bf16[2,8,9,1024]{3,1,2,0:T(8,128)(2,1)S(1)}, bf16[2,8,9,1024]{3,1,2,0:T(8,128)(2,1)S(1)}, u32[]{:S(2)}, u32[]{:S(2)}) collective-permute-start(bf16[2,8,9,1024]{3,1,2,0:T(8,128)(2,1)S(1)} %get-tuple-element.227), channel_id=1, source_target_pairs={{4,8},{8,4},{12,16},{16,12},{20,24},{24,20},{5,9},{9,5},{13,17},{1... | collective-permute-start | bytes 884744 | tf_op jit(solution)/shard_map/ppermute | solution.py:54
  10.8 83.0 %collective-permute-start.6 = (bf16[2,1024,512]{2,1,0:T(8,128)(2,1)}, bf16[2,1024,512]{2,1,0:T(8,128)(2,1)}, u32[]{:S(2)}, u32[]{:S(2)}) collective-permute-start(bf16[2,1024,512]{2,1,0:T(8,128)(2,1)} %get-tuple-element.220), channel_id=1, source_target_pairs={{0,3},{1,2},{2,1},{3,0},{4,7},{5,6},{6,5},{7,4},{8,11},{9,10},{10,... | collective-permute-start | bytes 6291464 | tf_op jit(solution)/shard_map/ppermute | solution.py:31
  11.4 4.5 %collective-permute-start = (f32[1024]{0:T(1024)S(1)}, f32[1024]{0:T(1024)S(1)}, u32[]{:S(2)}, u32[]{:S(2)}) collective-permute-start(f32[1024]{0:T(1024)S(1)} %bitcast.126), channel_id=1, source_target_pairs={{0,1},{1,0},{2,3},{3,2},{4,5},{5,4},{6,7},{7,6},{8,9},{9,8},{10,11... | collective-permute-start | bytes 12296 | tf_op jit(solution)/shard_map/ppermute | solution.py:31
  12.5 46.5 %collective-permute-start.1 = (f32[1024]{0:T(1024)S(1)}, f32[1024]{0:T(1024)S(1)}, u32[]{:S(2)}, u32[]{:S(2)}) collective-permute-start(f32[1024]{0:T(1024)S(1)} %bitcast.125), channel_id=1, source_target_pairs={{0,3},{1,2},{2,1},{3,0},{4,7},{5,6},{6,5},{7,4},{8,11},{9,10},{10,... | collective-permute-start | bytes 12296 | tf_op jit(solution)/shard_map/ppermute | solution.py:31
  16.0 79.2 %collective-permute-start.5 = (bf16[2,1024,512]{2,1,0:T(8,128)(2,1)}, bf16[2,1024,512]{2,1,0:T(8,128)(2,1)S(1)}, u32[]{:S(2)}, u32[]{:S(2)}) collective-permute-start(bf16[2,1024,512]{2,1,0:T(8,128)(2,1)} %get-tuple-element.221), channel_id=1, source_target_pairs={{0,1},{1,0},{2,3},{3,2},{4,5},{5,4},{6,7},{7,6},{8,9},{9,8},{10,11... | collective-permute-start | bytes 6291464 | tf_op jit(solution)/shard_map/ppermute | solution.py:31
  60.3 14.7 %collective-permute-start.8 = (bf16[2,40,1024]{2,0,1:T(2,128)(2,1)}, bf16[2,40,1024]{2,0,1:T(2,128)(2,1)S(1)}, u32[]{:S(2)}, u32[]{:S(2)}) collective-permute-start(bf16[2,40,1024]{2,0,1:T(2,128)(2,1)} %get-tuple-element.234), channel_id=1, source_target_pairs={{0,3},{1,2},{2,1},{3,0},{4,7},{5,6},{6,5},{7,4},{8,11},{9,10},{10,... | collective-permute-start | bytes 491528 | tf_op jit(solution)/shard_map/ppermute | solution.py:31
  66.9 8.6 %collective-permute-start.7 = (bf16[2,40,1024]{2,0,1:T(2,128)(2,1)}, bf16[2,40,1024]{2,0,1:T(2,128)(2,1)}, u32[]{:S(2)}, u32[]{:S(2)}) collective-permute-start(bf16[2,40,1024]{2,0,1:T(2,128)(2,1)} %get-tuple-element.235), channel_id=1, source_target_pairs={{0,1},{1,0},{2,3},{3,2},{4,5},{5,4},{6,7},{7,6},{8,9},{9,8},{10,11... | collective-permute-start | bytes 491528 | tf_op jit(solution)/shard_map/ppermute | solution.py:31
  74.5 11.5 %collective-permute-start.11 = (f32[2,41,1024]{2,1,0:T(8,128)}, f32[2,41,1024]{2,1,0:T(8,128)}, u32[]{:S(2)}, u32[]{:S(2)}) collective-permute-start(f32[2,41,1024]{2,1,0:T(8,128)} %get-tuple-element.224), channel_id=1, source_target_pairs={{0,3},{1,2},{2,1},{3,0},{4,7},{5,6},{6,5},{7,4},{8,11},{9,10},{10,... | collective-permute-start | bytes 1007624 | tf_op jit(solution)/shard_map/ppermute | solution.py:31
  75.0 11.7 %collective-permute-start.12 = (f32[2,41,1024]{2,1,0:T(8,128)}, f32[2,41,1024]{2,1,0:T(8,128)}, u32[]{:S(2)}, u32[]{:S(2)}) collective-permute-start(f32[2,41,1024]{2,1,0:T(8,128)} %get-tuple-element.225), channel_id=1, source_target_pairs={{0,1},{1,0},{2,3},{3,2},{4,5},{5,4},{6,7},{7,6},{8,9},{9,8},{10,11... | collective-permute-start | bytes 1007624 | tf_op jit(solution)/shard_map/ppermute | solution.py:31
  75.6 19.6 %collective-permute-start.2 = (bf16[40,512]{1,0:T(8,128)(2,1)S(1)}, bf16[40,512]{1,0:T(8,128)(2,1)S(1)}, u32[]{:S(2)}, u32[]{:S(2)}) collective-permute-start(bf16[40,512]{1,0:T(8,128)(2,1)S(1)} %concatenate.30.refs_1_), channel_id=1, source_target_pairs={{0,1},{1,0},{2,3},{3,2},{4,5},{5,4},{6,7},{7,6},{8,9},{9,8},{10,11... | collective-permute-start | bytes 122888 | tf_op jit(solution)/shard_map/ppermute | solution.py:31
  86.1 9.1 %collective-permute-start.3 = (bf16[40,512]{1,0:T(8,128)(2,1)S(1)}, bf16[40,512]{1,0:T(8,128)(2,1)S(1)}, u32[]{:S(2)}, u32[]{:S(2)}) collective-permute-start(bf16[40,512]{1,0:T(8,128)(2,1)S(1)} %concatenate.30.refs_1_), channel_id=1, source_target_pairs={{0,2},{1,3},{2,0},{3,1},{4,6},{5,7},{6,4},{7,5},{8,10},{9,11},{10,... | collective-permute-start | bytes 122888 | tf_op jit(solution)/shard_map/ppermute | solution.py:31
  86.7 8.5 %collective-permute-start.4 = (bf16[40,512]{1,0:T(8,128)(2,1)S(1)}, bf16[40,512]{1,0:T(8,128)(2,1)S(1)}, u32[]{:S(2)}, u32[]{:S(2)}) collective-permute-start(bf16[40,512]{1,0:T(8,128)(2,1)S(1)} %concatenate.30.refs_1_), channel_id=1, source_target_pairs={{0,3},{1,2},{2,1},{3,0},{4,7},{5,6},{6,5},{7,4},{8,11},{9,10},{10,... | collective-permute-start | bytes 122888 | tf_op jit(solution)/shard_map/ppermute | solution.py:31
  118.2 9.7 %collective-permute-start.13 = (bf16[40,512]{1,0:T(8,128)(2,1)S(1)}, bf16[40,512]{1,0:T(8,128)(2,1)S(1)}, u32[]{:S(2)}, u32[]{:S(2)}) collective-permute-start(bf16[40,512]{1,0:T(8,128)(2,1)S(1)} %get-tuple-element.101.refs_1_), channel_id=1, source_target_pairs={{0,1},{1,0},{2,3},{3,2},{4,5},{5,4},{6,7},{7,6},{8,9},{9,8},{10,11... | collective-permute-start | bytes 122888 | tf_op jit(solution)/shard_map/ppermute | solution.py:31
  120.6 7.3 %collective-permute-start.14 = (bf16[40,512]{1,0:T(8,128)(2,1)S(1)}, bf16[40,512]{1,0:T(8,128)(2,1)S(1)}, u32[]{:S(2)}, u32[]{:S(2)}) collective-permute-start(bf16[40,512]{1,0:T(8,128)(2,1)S(1)} %get-tuple-element.101.refs_1_), channel_id=1, source_target_pairs={{0,2},{1,3},{2,0},{3,1},{4,6},{5,7},{6,4},{7,5},{8,10},{9,11},{10,... | collective-permute-start | bytes 122888 | tf_op jit(solution)/shard_map/ppermute | solution.py:31
  120.6 7.3 %collective-permute-start.15 = (bf16[40,512]{1,0:T(8,128)(2,1)S(1)}, bf16[40,512]{1,0:T(8,128)(2,1)S(1)}, u32[]{:S(2)}, u32[]{:S(2)}) collective-permute-start(bf16[40,512]{1,0:T(8,128)(2,1)S(1)} %get-tuple-element.101.refs_1_), channel_id=1, source_target_pairs={{0,3},{1,2},{2,1},{3,0},{4,7},{5,6},{6,5},{7,4},{8,11},{9,10},{10,... | collective-permute-start | bytes 122888 | tf_op jit(solution)/shard_map/ppermute | solution.py:31
  122.1 5.6 %collective-permute-start.17 = (bf16[2,40,1024]{2,0,1:T(2,128)(2,1)S(1)}, bf16[2,40,1024]{2,0,1:T(2,128)(2,1)S(1)}, u32[]{:S(2)}, u32[]{:S(2)}) collective-permute-start(bf16[2,40,1024]{2,0,1:T(2,128)(2,1)S(1)} %copy.53), channel_id=1, source_target_pairs={{0,3},{1,2},{2,1},{3,0},{4,7},{5,6},{6,5},{7,4},{8,11},{9,10},{10,... | collective-permute-start | bytes 491528 | tf_op jit(solution)/shard_map/ppermute | solution.py:31
  122.6 5.3 %collective-permute-start.16 = (bf16[2,40,1024]{2,1,0:T(8,128)(2,1)S(1)}, bf16[2,40,1024]{2,1,0:T(8,128)(2,1)S(1)}, u32[]{:S(2)}, u32[]{:S(2)}) collective-permute-start(bf16[2,40,1024]{2,1,0:T(8,128)(2,1)S(1)} %get-tuple-element.105), channel_id=1, source_target_pairs={{0,1},{1,0},{2,3},{3,2},{4,5},{5,4},{6,7},{7,6},{8,9},{9,8},{10,11... | collective-permute-start | bytes 491528 | tf_op jit(solution)/shard_map/ppermute | solution.py:31
  147.9 9.4 %collective-permute-start.18 = (bf16[40,512]{1,0:T(8,128)(2,1)S(1)}, bf16[40,512]{1,0:T(8,128)(2,1)S(1)}, u32[]{:S(2)}, u32[]{:S(2)}) collective-permute-start(bf16[40,512]{1,0:T(8,128)(2,1)S(1)} %get-tuple-element.109.refs_1_), channel_id=1, source_target_pairs={{0,1},{1,0},{2,3},{3,2},{4,5},{5,4},{6,7},{7,6},{8,9},{9,8},{10,11... | collective-permute-start | bytes 122888 | tf_op jit(solution)/shard_map/ppermute | solution.py:31
  148.7 8.6 %collective-permute-start.19 = (bf16[40,512]{1,0:T(8,128)(2,1)S(1)}, bf16[40,512]{1,0:T(8,128)(2,1)S(1)}, u32[]{:S(2)}, u32[]{:S(2)}) collective-permute-start(bf16[40,512]{1,0:T(8,128)(2,1)S(1)} %get-tuple-element.109.refs_1_), channel_id=1, source_target_pairs={{0,2},{1,3},{2,0},{3,1},{4,6},{5,7},{6,4},{7,5},{8,10},{9,11},{10,... | collective-permute-start | bytes 122888 | tf_op jit(solution)/shard_map/ppermute | solution.py:31
  150.1 7.2 %collective-permute-start.20 = (bf16[40,512]{1,0:T(8,128)(2,1)S(1)}, bf16[40,512]{1,0:T(8,128)(2,1)S(1)}, u32[]{:S(2)}, u32[]{:S(2)}) collective-permute-start(bf16[40,512]{1,0:T(8,128)(2,1)S(1)} %get-tuple-element.109.refs_1_), channel_id=1, source_target_pairs={{0,3},{1,2},{2,1},{3,0},{4,7},{5,6},{6,5},{7,4},{8,11},{9,10},{10,... | collective-permute-start | bytes 122888 | tf_op jit(solution)/shard_map/ppermute | solution.py:31
  150.4 6.7 %collective-permute-start.22 = (bf16[2,40,1024]{2,0,1:T(2,128)(2,1)S(1)}, bf16[2,40,1024]{2,0,1:T(2,128)(2,1)S(1)}, u32[]{:S(2)}, u32[]{:S(2)}) collective-permute-start(bf16[2,40,1024]{2,0,1:T(2,128)(2,1)S(1)} %copy.55), channel_id=1, source_target_pairs={{0,3},{1,2},{2,1},{3,0},{4,7},{5,6},{6,5},{7,4},{8,11},{9,10},{10,... | collective-permute-start | bytes 491528 | tf_op jit(solution)/shard_map/ppermute | solution.py:31
  152.1 5.2 %collective-permute-start.21 = (bf16[2,40,1024]{2,1,0:T(8,128)(2,1)S(1)}, bf16[2,40,1024]{2,1,0:T(8,128)(2,1)S(1)}, u32[]{:S(2)}, u32[]{:S(2)}) collective-permute-start(bf16[2,40,1024]{2,1,0:T(8,128)(2,1)S(1)} %get-tuple-element.113), channel_id=1, source_target_pairs={{0,1},{1,0},{2,3},{3,2},{4,5},{5,4},{6,7},{7,6},{8,9},{9,8},{10,11... | collective-permute-start | bytes 491528 | tf_op jit(solution)/shard_map/ppermute | solution.py:31
  177.2 8.5 %collective-permute-start.23 = (bf16[40,512]{1,0:T(8,128)(2,1)S(1)}, bf16[40,512]{1,0:T(8,128)(2,1)S(1)}, u32[]{:S(2)}, u32[]{:S(2)}) collective-permute-start(bf16[40,512]{1,0:T(8,128)(2,1)S(1)} %get-tuple-element.117.refs_1_), channel_id=1, source_target_pairs={{0,1},{1,0},{2,3},{3,2},{4,5},{5,4},{6,7},{7,6},{8,9},{9,8},{10,11... | collective-permute-start | bytes 122888 | tf_op jit(solution)/shard_map/ppermute | solution.py:31
  177.4 8.3 %collective-permute-start.24 = (bf16[40,512]{1,0:T(8,128)(2,1)S(1)}, bf16[40,512]{1,0:T(8,128)(2,1)S(1)}, u32[]{:S(2)}, u32[]{:S(2)}) collective-permute-start(bf16[40,512]{1,0:T(8,128)(2,1)S(1)} %get-tuple-element.117.refs_1_), channel_id=1, source_target_pairs={{0,2},{1,3},{2,0},{3,1},{4,6},{5,7},{6,4},{7,5},{8,10},{9,11},{10,... | collective-permute-start | bytes 122888 | tf_op jit(solution)/shard_map/ppermute | solution.py:31
  178.6 7.1 %collective-permute-start.25 = (bf16[40,512]{1,0:T(8,128)(2,1)S(1)}, bf16[40,512]{1,0:T(8,128)(2,1)S(1)}, u32[]{:S(2)}, u32[]{:S(2)}) collective-permute-start(bf16[40,512]{1,0:T(8,128)(2,1)S(1)} %get-tuple-element.117.refs_1_), channel_id=1, source_target_pairs={{0,3},{1,2},{2,1},{3,0},{4,7},{5,6},{6,5},{7,4},{8,11},{9,10},{10,... | collective-permute-start | bytes 122888 | tf_op jit(solution)/shard_map/ppermute | solution.py:31
  179.2 6.3 %collective-permute-start.27 = (bf16[2,40,1024]{2,0,1:T(2,128)(2,1)S(1)}, bf16[2,40,1024]{2,0,1:T(2,128)(2,1)S(1)}, u32[]{:S(2)}, u32[]{:S(2)}) collective-permute-start(bf16[2,40,1024]{2,0,1:T(2,128)(2,1)S(1)} %copy.57), channel_id=1, source_target_pairs={{0,3},{1,2},{2,1},{3,0},{4,7},{5,6},{6,5},{7,4},{8,11},{9,10},{10,... | collective-permute-start | bytes 491528 | tf_op jit(solution)/shard_map/ppermute | solution.py:31
  180.6 5.1 %collective-permute-start.26 = (bf16[2,40,1024]{2,1,0:T(8,128)(2,1)S(1)}, bf16[2,40,1024]{2,1,0:T(8,128)(2,1)S(1)}, u32[]{:S(2)}, u32[]{:S(2)}) collective-permute-start(bf16[2,40,1024]{2,1,0:T(8,128)(2,1)S(1)} %get-tuple-element.121), channel_id=1, source_target_pairs={{0,1},{1,0},{2,3},{3,2},{4,5},{5,4},{6,7},{7,6},{8,9},{9,8},{10,11... | collective-permute-start | bytes 491528 | tf_op jit(solution)/shard_map/ppermute | solution.py:31
  205.9 8.2 %collective-permute-start.28 = (bf16[40,512]{1,0:T(8,128)(2,1)S(1)}, bf16[40,512]{1,0:T(8,128)(2,1)S(1)}, u32[]{:S(2)}, u32[]{:S(2)}) collective-permute-start(bf16[40,512]{1,0:T(8,128)(2,1)S(1)} %get-tuple-element.125.refs_1_), channel_id=1, source_target_pairs={{0,1},{1,0},{2,3},{3,2},{4,5},{5,4},{6,7},{7,6},{8,9},{9,8},{10,11... | collective-permute-start | bytes 122888 | tf_op jit(solution)/shard_map/ppermute | solution.py:31
  206.2 7.9 %collective-permute-start.29 = (bf16[40,512]{1,0:T(8,128)(2,1)S(1)}, bf16[40,512]{1,0:T(8,128)(2,1)S(1)}, u32[]{:S(2)}, u32[]{:S(2)}) collective-permute-start(bf16[40,512]{1,0:T(8,128)(2,1)S(1)} %get-tuple-element.125.refs_1_), channel_id=1, source_target_pairs={{0,2},{1,3},{2,0},{3,1},{4,6},{5,7},{6,4},{7,5},{8,10},{9,11},{10,... | collective-permute-start | bytes 122888 | tf_op jit(solution)/shard_map/ppermute | solution.py:31
  207.2 6.9 %collective-permute-start.30 = (bf16[40,512]{1,0:T(8,128)(2,1)S(1)}, bf16[40,512]{1,0:T(8,128)(2,1)S(1)}, u32[]{:S(2)}, u32[]{:S(2)}) collective-permute-start(bf16[40,512]{1,0:T(8,128)(2,1)S(1)} %get-tuple-element.125.refs_1_), channel_id=1, source_target_pairs={{0,3},{1,2},{2,1},{3,0},{4,7},{5,6},{6,5},{7,4},{8,11},{9,10},{10,... | collective-permute-start | bytes 122888 | tf_op jit(solution)/shard_map/ppermute | solution.py:31
  207.9 6.0 %collective-permute-start.32 = (bf16[2,40,1024]{2,0,1:T(2,128)(2,1)S(1)}, bf16[2,40,1024]{2,0,1:T(2,128)(2,1)S(1)}, u32[]{:S(2)}, u32[]{:S(2)}) collective-permute-start(bf16[2,40,1024]{2,0,1:T(2,128)(2,1)S(1)} %copy.59), channel_id=1, source_target_pairs={{0,3},{1,2},{2,1},{3,0},{4,7},{5,6},{6,5},{7,4},{8,11},{9,10},{10,... | collective-permute-start | bytes 491528 | tf_op jit(solution)/shard_map/ppermute | solution.py:31
  209.1 4.9 %collective-permute-start.31 = (bf16[2,40,1024]{2,1,0:T(8,128)(2,1)S(1)}, bf16[2,40,1024]{2,1,0:T(8,128)(2,1)S(1)}, u32[]{:S(2)}, u32[]{:S(2)}) collective-permute-start(bf16[2,40,1024]{2,1,0:T(8,128)(2,1)S(1)} %get-tuple-element.129), channel_id=1, source_target_pairs={{0,1},{1,0},{2,3},{3,2},{4,5},{5,4},{6,7},{7,6},{8,9},{9,8},{10,11... | collective-permute-start | bytes 491528 | tf_op jit(solution)/shard_map/ppermute | solution.py:31
  234.0 8.4 %collective-permute-start.33 = (bf16[40,512]{1,0:T(8,128)(2,1)S(1)}, bf16[40,512]{1,0:T(8,128)(2,1)S(1)}, u32[]{:S(2)}, u32[]{:S(2)}) collective-permute-start(bf16[40,512]{1,0:T(8,128)(2,1)S(1)} %get-tuple-element.133.refs_1_), channel_id=1, source_target_pairs={{0,1},{1,0},{2,3},{3,2},{4,5},{5,4},{6,7},{7,6},{8,9},{9,8},{10,11... | collective-permute-start | bytes 122888 | tf_op jit(solution)/shard_map/ppermute | solution.py:31
  234.5 7.9 %collective-permute-start.34 = (bf16[40,512]{1,0:T(8,128)(2,1)S(1)}, bf16[40,512]{1,0:T(8,128)(2,1)S(1)}, u32[]{:S(2)}, u32[]{:S(2)}) collective-permute-start(bf16[40,512]{1,0:T(8,128)(2,1)S(1)} %get-tuple-element.133.refs_1_), channel_id=1, source_target_pairs={{0,2},{1,3},{2,0},{3,1},{4,6},{5,7},{6,4},{7,5},{8,10},{9,11},{10,... | collective-permute-start | bytes 122888 | tf_op jit(solution)/shard_map/ppermute | solution.py:31
  235.5 6.9 %collective-permute-start.35 = (bf16[40,512]{1,0:T(8,128)(2,1)S(1)}, bf16[40,512]{1,0:T(8,128)(2,1)S(1)}, u32[]{:S(2)}, u32[]{:S(2)}) collective-permute-start(bf16[40,512]{1,0:T(8,128)(2,1)S(1)} %get-tuple-element.133.refs_1_), channel_id=1, source_target_pairs={{0,3},{1,2},{2,1},{3,0},{4,7},{5,6},{6,5},{7,4},{8,11},{9,10},{10,... | collective-permute-start | bytes 122888 | tf_op jit(solution)/shard_map/ppermute | solution.py:31
  236.0 6.2 %collective-permute-start.37 = (bf16[2,40,1024]{2,0,1:T(2,128)(2,1)S(1)}, bf16[2,40,1024]{2,0,1:T(2,128)(2,1)S(1)}, u32[]{:S(2)}, u32[]{:S(2)}) collective-permute-start(bf16[2,40,1024]{2,0,1:T(2,128)(2,1)S(1)} %copy.61), channel_id=1, source_target_pairs={{0,3},{1,2},{2,1},{3,0},{4,7},{5,6},{6,5},{7,4},{8,11},{9,10},{10,... | collective-permute-start | bytes 491528 | tf_op jit(solution)/shard_map/ppermute | solution.py:31
  237.5 4.9 %collective-permute-start.36 = (bf16[2,40,1024]{2,1,0:T(8,128)(2,1)S(1)}, bf16[2,40,1024]{2,1,0:T(8,128)(2,1)S(1)}, u32[]{:S(2)}, u32[]{:S(2)}) collective-permute-start(bf16[2,40,1024]{2,1,0:T(8,128)(2,1)S(1)} %get-tuple-element.137), channel_id=1, source_target_pairs={{0,1},{1,0},{2,3},{3,2},{4,5},{5,4},{6,7},{7,6},{8,9},{9,8},{10,11... | collective-permute-start | bytes 491528 | tf_op jit(solution)/shard_map/ppermute | solution.py:31
  262.3 8.4 %collective-permute-start.38 = (bf16[40,512]{1,0:T(8,128)(2,1)S(1)}, bf16[40,512]{1,0:T(8,128)(2,1)S(1)}, u32[]{:S(2)}, u32[]{:S(2)}) collective-permute-start(bf16[40,512]{1,0:T(8,128)(2,1)S(1)} %get-tuple-element.141.refs_1_), channel_id=1, source_target_pairs={{0,1},{1,0},{2,3},{3,2},{4,5},{5,4},{6,7},{7,6},{8,9},{9,8},{10,11... | collective-permute-start | bytes 122888 | tf_op jit(solution)/shard_map/ppermute | solution.py:31
  262.8 7.9 %collective-permute-start.39 = (bf16[40,512]{1,0:T(8,128)(2,1)S(1)}, bf16[40,512]{1,0:T(8,128)(2,1)S(1)}, u32[]{:S(2)}, u32[]{:S(2)}) collective-permute-start(bf16[40,512]{1,0:T(8,128)(2,1)S(1)} %get-tuple-element.141.refs_1_), channel_id=1, source_target_pairs={{0,2},{1,3},{2,0},{3,1},{4,6},{5,7},{6,4},{7,5},{8,10},{9,11},{10,... | collective-permute-start | bytes 122888 | tf_op jit(solution)/shard_map/ppermute | solution.py:31
  263.8 6.9 %collective-permute-start.40 = (bf16[40,512]{1,0:T(8,128)(2,1)S(1)}, bf16[40,512]{1,0:T(8,128)(2,1)S(1)}, u32[]{:S(2)}, u32[]{:S(2)}) collective-permute-start(bf16[40,512]{1,0:T(8,128)(2,1)S(1)} %get-tuple-element.141.refs_1_), channel_id=1, source_target_pairs={{0,3},{1,2},{2,1},{3,0},{4,7},{5,6},{6,5},{7,4},{8,11},{9,10},{10,... | collective-permute-start | bytes 122888 | tf_op jit(solution)/shard_map/ppermute | solution.py:31
  264.4 6.2 %collective-permute-start.42 = (bf16[2,40,1024]{2,0,1:T(2,128)(2,1)S(1)}, bf16[2,40,1024]{2,0,1:T(2,128)(2,1)S(1)}, u32[]{:S(2)}, u32[]{:S(2)}) collective-permute-start(bf16[2,40,1024]{2,0,1:T(2,128)(2,1)S(1)} %copy.63), channel_id=1, source_target_pairs={{0,3},{1,2},{2,1},{3,0},{4,7},{5,6},{6,5},{7,4},{8,11},{9,10},{10,... | collective-permute-start | bytes 491528 | tf_op jit(solution)/shard_map/ppermute | solution.py:31
  265.8 4.9 %collective-permute-start.41 = (bf16[2,40,1024]{2,1,0:T(8,128)(2,1)S(1)}, bf16[2,40,1024]{2,1,0:T(8,128)(2,1)S(1)}, u32[]{:S(2)}, u32[]{:S(2)}) collective-permute-start(bf16[2,40,1024]{2,1,0:T(8,128)(2,1)S(1)} %get-tuple-element.145), channel_id=1, source_target_pairs={{0,1},{1,0},{2,3},{3,2},{4,5},{5,4},{6,7},{7,6},{8,9},{9,8},{10,11... | collective-permute-start | bytes 491528 | tf_op jit(solution)/shard_map/ppermute | solution.py:31
  290.6 8.4 %collective-permute-start.43 = (bf16[40,512]{1,0:T(8,128)(2,1)S(1)}, bf16[40,512]{1,0:T(8,128)(2,1)S(1)}, u32[]{:S(2)}, u32[]{:S(2)}) collective-permute-start(bf16[40,512]{1,0:T(8,128)(2,1)S(1)} %get-tuple-element.149.refs_1_), channel_id=1, source_target_pairs={{0,1},{1,0},{2,3},{3,2},{4,5},{5,4},{6,7},{7,6},{8,9},{9,8},{10,11... | collective-permute-start | bytes 122888 | tf_op jit(solution)/shard_map/ppermute | solution.py:31
  291.1 7.9 %collective-permute-start.44 = (bf16[40,512]{1,0:T(8,128)(2,1)S(1)}, bf16[40,512]{1,0:T(8,128)(2,1)S(1)}, u32[]{:S(2)}, u32[]{:S(2)}) collective-permute-start(bf16[40,512]{1,0:T(8,128)(2,1)S(1)} %get-tuple-element.149.refs_1_), channel_id=1, source_target_pairs={{0,2},{1,3},{2,0},{3,1},{4,6},{5,7},{6,4},{7,5},{8,10},{9,11},{10,... | collective-permute-start | bytes 122888 | tf_op jit(solution)/shard_map/ppermute | solution.py:31
  292.1 6.9 %collective-permute-start.45 = (bf16[40,512]{1,0:T(8,128)(2,1)S(1)}, bf16[40,512]{1,0:T(8,128)(2,1)S(1)}, u32[]{:S(2)}, u32[]{:S(2)}) collective-permute-start(bf16[40,512]{1,0:T(8,128)(2,1)S(1)} %get-tuple-element.149.refs_1_), channel_id=1, source_target_pairs={{0,3},{1,2},{2,1},{3,0},{4,7},{5,6},{6,5},{7,4},{8,11},{9,10},{10,... | collective-permute-start | bytes 122888 | tf_op jit(solution)/shard_map/ppermute | solution.py:31
  292.7 6.2 %collective-permute-start.47 = (bf16[2,40,1024]{2,0,1:T(2,128)(2,1)S(1)}, bf16[2,40,1024]{2,0,1:T(2,128)(2,1)S(1)}, u32[]{:S(2)}, u32[]{:S(2)}) collective-permute-start(bf16[2,40,1024]{2,0,1:T(2,128)(2,1)S(1)} %copy.65), channel_id=1, source_target_pairs={{0,3},{1,2},{2,1},{3,0},{4,7},{5,6},{6,5},{7,4},{8,11},{9,10},{10,... | collective-permute-start | bytes 491528 | tf_op jit(solution)/shard_map/ppermute | solution.py:31
  294.1 4.9 %collective-permute-start.46 = (bf16[2,40,1024]{2,1,0:T(8,128)(2,1)S(1)}, bf16[2,40,1024]{2,1,0:T(8,128)(2,1)S(1)}, u32[]{:S(2)}, u32[]{:S(2)}) collective-permute-start(bf16[2,40,1024]{2,1,0:T(8,128)(2,1)S(1)} %get-tuple-element.153), channel_id=1, source_target_pairs={{0,1},{1,0},{2,3},{3,2},{4,5},{5,4},{6,7},{7,6},{8,9},{9,8},{10,11... | collective-permute-start | bytes 491528 | tf_op jit(solution)/shard_map/ppermute | solution.py:31
  319.1 8.4 %collective-permute-start.48 = (bf16[40,512]{1,0:T(8,128)(2,1)S(1)}, bf16[40,512]{1,0:T(8,128)(2,1)S(1)}, u32[]{:S(2)}, u32[]{:S(2)}) collective-permute-start(bf16[40,512]{1,0:T(8,128)(2,1)S(1)} %get-tuple-element.157.refs_1_), channel_id=1, source_target_pairs={{0,1},{1,0},{2,3},{3,2},{4,5},{5,4},{6,7},{7,6},{8,9},{9,8},{10,11... | collective-permute-start | bytes 122888 | tf_op jit(solution)/shard_map/ppermute | solution.py:31
  319.6 7.9 %collective-permute-start.49 = (bf16[40,512]{1,0:T(8,128)(2,1)S(1)}, bf16[40,512]{1,0:T(8,128)(2,1)S(1)}, u32[]{:S(2)}, u32[]{:S(2)}) collective-permute-start(bf16[40,512]{1,0:T(8,128)(2,1)S(1)} %get-tuple-element.157.refs_1_), channel_id=1, source_target_pairs={{0,2},{1,3},{2,0},{3,1},{4,6},{5,7},{6,4},{7,5},{8,10},{9,11},{10,... | collective-permute-start | bytes 122888 | tf_op jit(solution)/shard_map/ppermute | solution.py:31
  320.6 6.9 %collective-permute-start.50 = (bf16[40,512]{1,0:T(8,128)(2,1)S(1)}, bf16[40,512]{1,0:T(8,128)(2,1)S(1)}, u32[]{:S(2)}, u32[]{:S(2)}) collective-permute-start(bf16[40,512]{1,0:T(8,128)(2,1)S(1)} %get-tuple-element.157.refs_1_), channel_id=1, source_target_pairs={{0,3},{1,2},{2,1},{3,0},{4,7},{5,6},{6,5},{7,4},{8,11},{9,10},{10,... | collective-permute-start | bytes 122888 | tf_op jit(solution)/shard_map/ppermute | solution.py:31
  321.1 6.2 %collective-permute-start.52 = (bf16[2,40,1024]{2,0,1:T(2,128)(2,1)S(1)}, bf16[2,40,1024]{2,0,1:T(2,128)(2,1)S(1)}, u32[]{:S(2)}, u32[]{:S(2)}) collective-permute-start(bf16[2,40,1024]{2,0,1:T(2,128)(2,1)S(1)} %copy.67), channel_id=1, source_target_pairs={{0,3},{1,2},{2,1},{3,0},{4,7},{5,6},{6,5},{7,4},{8,11},{9,10},{10,... | collective-permute-start | bytes 491528 | tf_op jit(solution)/shard_map/ppermute | solution.py:31
  322.6 4.9 %collective-permute-start.51 = (bf16[2,40,1024]{2,1,0:T(8,128)(2,1)S(1)}, bf16[2,40,1024]{2,1,0:T(8,128)(2,1)S(1)}, u32[]{:S(2)}, u32[]{:S(2)}) collective-permute-start(bf16[2,40,1024]{2,1,0:T(8,128)(2,1)S(1)} %get-tuple-element.161), channel_id=1, source_target_pairs={{0,1},{1,0},{2,3},{3,2},{4,5},{5,4},{6,7},{7,6},{8,9},{9,8},{10,11... | collective-permute-start | bytes 491528 | tf_op jit(solution)/shard_map/ppermute | solution.py:31
  346.5 8.4 %collective-permute-start.53 = (bf16[40,512]{1,0:T(8,128)(2,1)S(1)}, bf16[40,512]{1,0:T(8,128)(2,1)S(1)}, u32[]{:S(2)}, u32[]{:S(2)}) collective-permute-start(bf16[40,512]{1,0:T(8,128)(2,1)S(1)} %get-tuple-element.165), channel_id=1, source_target_pairs={{0,1},{1,0},{2,3},{3,2},{4,5},{5,4},{6,7},{7,6},{8,9},{9,8},{10,11... | collective-permute-start | bytes 122888 | tf_op jit(solution)/shard_map/ppermute | solution.py:31
  347.0 7.9 %collective-permute-start.54 = (bf16[40,512]{1,0:T(8,128)(2,1)S(1)}, bf16[40,512]{1,0:T(8,128)(2,1)S(1)}, u32[]{:S(2)}, u32[]{:S(2)}) collective-permute-start(bf16[40,512]{1,0:T(8,128)(2,1)S(1)} %get-tuple-element.165), channel_id=1, source_target_pairs={{0,2},{1,3},{2,0},{3,1},{4,6},{5,7},{6,4},{7,5},{8,10},{9,11},{10,... | collective-permute-start | bytes 122888 | tf_op jit(solution)/shard_map/ppermute | solution.py:31
  348.0 6.9 %collective-permute-start.55 = (bf16[40,512]{1,0:T(8,128)(2,1)S(1)}, bf16[40,512]{1,0:T(8,128)(2,1)S(1)}, u32[]{:S(2)}, u32[]{:S(2)}) collective-permute-start(bf16[40,512]{1,0:T(8,128)(2,1)S(1)} %get-tuple-element.165), channel_id=1, source_target_pairs={{0,3},{1,2},{2,1},{3,0},{4,7},{5,6},{6,5},{7,4},{8,11},{9,10},{10,... | collective-permute-start | bytes 122888 | tf_op jit(solution)/shard_map/ppermute | solution.py:31
  348.5 6.2 %collective-permute-start.57 = (bf16[2,40,1024]{2,0,1:T(2,128)(2,1)S(1)}, bf16[2,40,1024]{2,0,1:T(2,128)(2,1)S(1)}, u32[]{:S(2)}, u32[]{:S(2)}) collective-permute-start(bf16[2,40,1024]{2,0,1:T(2,128)(2,1)S(1)} %copy.69), channel_id=1, source_target_pairs={{0,3},{1,2},{2,1},{3,0},{4,7},{5,6},{6,5},{7,4},{8,11},{9,10},{10,... | collective-permute-start | bytes 491528 | tf_op jit(solution)/shard_map/ppermute | solution.py:31
  350.0 4.9 %collective-permute-start.56 = (bf16[2,40,1024]{2,1,0:T(8,128)(2,1)S(1)}, bf16[2,40,1024]{2,1,0:T(8,128)(2,1)S(1)}, u32[]{:S(2)}, u32[]{:S(2)}) collective-permute-start(bf16[2,40,1024]{2,1,0:T(8,128)(2,1)S(1)} %get-tuple-element.169), channel_id=1, source_target_pairs={{0,1},{1,0},{2,3},{3,2},{4,5},{5,4},{6,7},{7,6},{8,9},{9,8},{10,11... | collective-permute-start | bytes 491528 | tf_op jit(solution)/shard_map/ppermute | solution.py:31
  365.2 8.3 %collective-permute-start.58 = (f32[12,1024]{1,0:T(8,128)S(1)}, f32[12,1024]{1,0:T(8,128)S(1)}, u32[]{:S(2)}, u32[]{:S(2)}) collective-permute-start(f32[12,1024]{1,0:T(8,128)S(1)} %bitcast.120), channel_id=1, source_target_pairs={{0,4},{4,0},{8,12},{12,8},{16,20},{20,16},{24,28},{28,24},{1,5},{5... | collective-permute-start | bytes 147464 | tf_op jit(solution)/shard_map/ppermute | solution.py:31
  369.2 7.6 %collective-permute-start.59 = (f32[12,1024]{1,0:T(8,128)S(1)}, f32[12,1024]{1,0:T(8,128)S(1)}, u32[]{:S(2)}, u32[]{:S(2)}) collective-permute-start(f32[12,1024]{1,0:T(8,128)S(1)} %bitcast.121), channel_id=1, source_target_pairs={{0,28},{4,24},{8,20},{12,16},{16,12},{20,8},{24,4},{28,0},{1,29},{... | collective-permute-start | bytes 147464 | tf_op jit(solution)/shard_map/ppermute | solution.py:31
  371.6 6.0 %collective-permute-start.60 = (f32[12,1024]{1,0:T(8,128)S(1)}, f32[12,1024]{1,0:T(8,128)S(1)}, u32[]{:S(2)}, u32[]{:S(2)}) collective-permute-start(f32[12,1024]{1,0:T(8,128)S(1)} %bitcast.122), channel_id=1, source_target_pairs={{0,12},{4,8},{8,4},{12,0},{16,28},{20,24},{24,20},{28,16},{1,13},{... | collective-permute-start | bytes 147464 | tf_op jit(solution)/shard_map/ppermute | solution.py:31
  384.5 3.6 collective-permute-start.62
  388.1 3.6 collective-permute-start.63
  395.4 5.8 %collective-permute-start.65 = (f32[8,128]{1,0:T(8,128)S(1)}, f32[8,128]{1,0:T(8,128)S(1)}, u32[]{:S(2)}, u32[]{:S(2)}) collective-permute-start(f32[8,128]{1,0:T(8,128)S(1)} %add.195), channel_id=1, source_target_pairs={{0,16},{4,20},{8,24},{12,28},{16,0},{20,4},{24,8},{28,12},{1,17},{... | collective-permute-start | bytes 12296 | tf_op jit(solution)/shard_map/ppermute | solution.py:31
  (20 other events, 133.9 us)
